TPU v7x, 8 devices: a whole 2x2x1 slice. The times are simulated.
8 devices in a mesh: third: 2 (over z, y), second: 2 (over x), group: 2 (over core).
Axes of the slice: x: 2, y: 2, z: 1, core: 2. Of those that a mesh axis runs over, the one named last changes fastest.
Arguments:
- x_one: bfloat16 [65536, 768], P(('third', 'second', 'group'))
- z_one: bfloat16 [65536, 3072], P(('third', 'second', 'group'))
- x_two: bfloat16 [65536, 768], P(('third', 'second', 'group'))
- z_two: bfloat16 [65536, 3072], P(('third', 'second', 'group'))
- grad_out: bfloat16 [65536, 768], P(('third', 'second', 'group'))
- w1_in: bfloat16 [768, 3072], replicated
- w1_out: bfloat16 [3072, 768], replicated
- w2_in: bfloat16 [768, 3072], replicated
- w2_out: bfloat16 [3072, 768], replicated
Outputs:
- output 1: float32 [3072, 768], replicated
- output 2: float32 [768, 3072], replicated
- output 3: float32 [3072, 768], replicated
- output 4: float32 [768, 3072], replicated
- output 5: bfloat16 [65536, 768], P(('third', 'second', 'group'))
All inputs are finite; a program needn't handle non-finite values.
Results may differ from a plain program's by a relative error of at most 0.00508575.
Values are sent between devices in bfloat16 or wider.
A program may use at most 1 GiB of HBM per device.

v0:
```python
import math
import jax
import jax.numpy as jnp
from jax import lax
from jax.sharding import PartitionSpec as P

AXES = ('third', 'second', 'group')
INV_ROOT_TWO = math.sqrt(0.5)
INV_ROOT_TWO_PI = 1.0 / math.sqrt(2.0 * math.pi)
CONTRACT_ROWS = (((0,), (0,)), ((), ()))
CONTRACT_COLS = (((1,), (1,)), ((), ()))


def gelu_pair(z_pre):
    z_val = z_pre.astype(jnp.float32)
    cdf_val = 0.5 * (1.0 + lax.erf(z_val * INV_ROOT_TWO))
    hidden = (z_val * cdf_val).astype(jnp.bfloat16)
    slope = cdf_val + z_val * jnp.exp(-0.5 * z_val * z_val) * INV_ROOT_TWO_PI
    return hidden, slope


def block_backward(x_in, z_pre, grad_y, w_in, w_out):
    hidden, slope = gelu_pair(z_pre)
    w_out_grad = lax.dot_general(hidden, grad_y, CONTRACT_ROWS, preferred_element_type=jnp.float32).astype(jnp.bfloat16)
    grad_hidden = lax.dot_general(grad_y, w_out, CONTRACT_COLS, preferred_element_type=jnp.float32)
    grad_pre = (grad_hidden * slope).astype(jnp.bfloat16)
    w_in_grad = lax.dot_general(x_in, grad_pre, CONTRACT_ROWS, preferred_element_type=jnp.float32).astype(jnp.bfloat16)
    grad_x = (grad_y.astype(jnp.float32) + lax.dot_general(grad_pre, w_in, CONTRACT_COLS, preferred_element_type=jnp.float32)).astype(jnp.bfloat16)
    return w_out_grad, w_in_grad, grad_x


def reduce_grad(grad, group_size):
    row_count, col_count = grad.shape
    pieces = grad.reshape(group_size, row_count // group_size, col_count)
    received = lax.all_to_all(pieces, 'group', 0, 0)
    part_sum = jnp.sum(received, axis=0, dtype=jnp.float32)
    part_sum = lax.psum_scatter(part_sum, 'second', scatter_dimension=0, tiled=True)
    part_sum = lax.psum_scatter(part_sum, 'third', scatter_dimension=0, tiled=True)
    full_sum = lax.all_gather(part_sum, 'third', axis=0, tiled=True)
    full_sum = lax.all_gather(full_sum, 'second', axis=0, tiled=True)
    return lax.all_gather(full_sum, 'group', axis=0, tiled=True)


def solution(mesh):
    group_size = mesh.shape['group']

    def device_step(x_one, z_one, x_two, z_two, grad_out, w1_in, w1_out, w2_in, w2_out):
        w2o_grad, w2i_grad, dx_two = block_backward(x_two, z_two, grad_out, w2_in, w2_out)
        sum_w2o = reduce_grad(w2o_grad, group_size)
        sum_w2i = reduce_grad(w2i_grad, group_size)
        w1o_grad, w1i_grad, dx_one = block_backward(x_one, z_one, dx_two, w1_in, w1_out)
        sum_w1o = reduce_grad(w1o_grad, group_size)
        sum_w1i = reduce_grad(w1i_grad, group_size)
        return sum_w2o, sum_w2i, sum_w1o, sum_w1i, dx_one

    row_spec = P(AXES, None)
    repl_spec = P()
    return jax.shard_map(
        device_step,
        mesh=mesh,
        in_specs=(row_spec, row_spec, row_spec, row_spec, row_spec, repl_spec, repl_spec, repl_spec, repl_spec),
        out_specs=(repl_spec, repl_spec, repl_spec, repl_spec, row_spec),
        check_vma=False,
    )
```

profile of v0, /device:TPU:0, one launch (start us, length us, event | category | flops | bytes accessed | tf_op | source)
XLA Modules:
  0.0 1179.2 jit_solution(10618943985561212475)
XLA Ops:
  7.2 0.0 reduce-scatter.9.cloned.1.call-start
  7.2 54.8 %fusion.22 = bf16[3072,768]{1,0:T(8,128)(2,1)} fusion(bf16[8192,768]{1,0:T(8,128)(2,1)} %param.13, bf16[8192,3072]{1,0:T(8,128)(2,1)} %param.12), kind=kOutput, calls=%fused_computation.36 | convolution fusion | flops 38808059904 | bytes 67633152 | tf_op jit(solution)/shard_map/dot_general | solution.py:24
  62.0 9.4 all_to_all.20
  71.4 3.0 convert_reduce_fusion.3
  74.4 0.0 reduce-scatter.9.cloned.1.call-update
  74.4 0.0 reduce-scatter.13.cloned.1.call-start
  74.5 78.3 %fusion.8 = bf16[8192,3072]{1,0:T(8,128)(2,1)} fusion(bf16[8192,3072]{1,0:T(8,128)(2,1)} %param.12, bf16[8192,768]{1,0:T(8,128)(2,1)} %param.13, bf16[3072,768]{1,0:T(8,128)(2,1)} %param.17), kind=kOutput, calls=%fused_computation.18 | convolution fusion | flops 38931529728 | bytes 117964800 | tf_op jit(solution)/shard_map/dot_general | solution.py:25
  152.8 48.1 %convolution_convert_fusion.1 = bf16[3072,768]{0,1:T(8,128)(2,1)} fusion(bf16[8192,3072]{1,0:T(8,128)(2,1)} %fusion.8, bf16[8192,768]{1,0:T(8,128)(2,1)} %param.11), kind=kOutput, calls=%fused_computation.39 | convolution fusion | flops 38657064960 | bytes 67633152 | tf_op jit(solution)/shard_map/dot_general | solution.py:27
  200.8 8.8 all_to_all.21
  209.6 3.2 convert_reduce_fusion.2
  212.9 0.0 reduce-scatter.17.cloned.1.call-start
  212.9 47.4 %add_convert_fusion.1 = bf16[8192,768]{1,0:T(8,128)(2,1)} fusion(bf16[8192,768]{1,0:T(8,128)(2,1)} %param.13, bf16[8192,3072]{1,0:T(8,128)(2,1)} %fusion.8, bf16[768,3072]{1,0:T(8,128)(2,1)} %param.16), kind=kOutput, calls=%fused_computation.31 | convolution fusion | flops 38673580032 | bytes 80216064 | tf_op jit(solution)/shard_map/dot_general | solution.py:28
  260.4 63.3 %fusion.25 = bf16[3072,768]{1,0:T(8,128)(2,1)} fusion(bf16[8192,768]{1,0:T(8,128)(2,1)} %add_convert_fusion.1, bf16[8192,3072]{1,0:T(8,128)(2,1)} %param.10), kind=kOutput, calls=%fused_computation.37 | convolution fusion | flops 38808059904 | bytes 67633152 | tf_op jit(solution)/shard_map/dot_general | solution.py:24
  323.7 8.8 all_to_all.22
  332.4 3.0 convert_reduce_fusion.1
  335.5 0.0 reduce-scatter.21.cloned.1.call-start
  335.5 78.5 %fusion.17 = bf16[8192,3072]{1,0:T(8,128)(2,1)} fusion(bf16[8192,3072]{1,0:T(8,128)(2,1)} %param.10, bf16[8192,768]{1,0:T(8,128)(2,1)} %add_convert_fusion.1, bf16[3072,768]{1,0:T(8,128)(2,1)} %param.15), kind=kOutput, calls=%fused_computation.27 | convolution fusion | flops 38931529728 | bytes 117964800 | tf_op jit(solution)/shard_map/dot_general | solution.py:25
  414.0 48.1 %convolution_convert_fusion = bf16[3072,768]{0,1:T(8,128)(2,1)} fusion(bf16[8192,3072]{1,0:T(8,128)(2,1)} %fusion.17, bf16[8192,768]{1,0:T(8,128)(2,1)} %param.9), kind=kOutput, calls=%fused_computation.38 | convolution fusion | flops 38657064960 | bytes 67633152 | tf_op jit(solution)/shard_map/dot_general | solution.py:27
  462.1 8.8 all_to_all.23
  470.8 3.2 convert_reduce_fusion
  474.1 0.0 reduce-scatter.11.cloned.1.call-start
  474.2 0.0 reduce-scatter.9.cloned.1.call-done
  474.2 0.5 reduce-scatter.11.cloned.1.call-update
  474.7 0.0 reduce-scatter.15.cloned.1.call-start
  474.8 0.0 reduce-scatter.13.cloned.1.call-done
  474.8 0.5 reduce-scatter.15.cloned.1.call-update
  475.3 0.0 reduce-scatter.19.cloned.1.call-start
  475.3 0.0 reduce-scatter.17.cloned.1.call-done
  475.4 0.7 reduce-scatter.19.cloned.1.call-update
  476.0 0.0 reduce-scatter.23.cloned.1.call-start
  476.1 57.9 %reduce-scatter.21.cloned.1.call-done = f32[192,3072]{1,0:T(8,128)} async-done(((f32[384,3072]{1,0:T(8,128)}), f32[192,3072]{1,0:T(8,128)}) %reduce-scatter.21.cloned.1.call-update) | async-done | bytes 2359312 | tf_op jit(solution)/shard_map/reduce_scatter | solution.py:37
  534.0 0.0 all-gather.13.cloned.1.call-start
  534.0 33.9 %reduce-scatter.11.cloned.1.call-done = f32[384,768]{1,0:T(8,128)} async-done(((f32[768,768]{1,0:T(8,128)}), f32[384,768]{1,0:T(8,128)}) %reduce-scatter.11.cloned.1.call-update) | async-done | bytes 1179664 | tf_op jit(solution)/shard_map/reduce_scatter | solution.py:38
  567.9 0.0 all-gather.19.cloned.1.call-start
  568.0 33.9 %reduce-scatter.15.cloned.1.call-done = f32[96,3072]{1,0:T(8,128)} async-done(((f32[192,3072]{1,0:T(8,128)}), f32[96,3072]{1,0:T(8,128)}) %reduce-scatter.15.cloned.1.call-update) | async-done | bytes 1179664 | tf_op jit(solution)/shard_map/reduce_scatter | solution.py:38
  602.0 0.0 all-gather.25.cloned.1.call-start
  602.0 34.1 %reduce-scatter.19.cloned.1.call-done = f32[384,768]{1,0:T(8,128)} async-done(((f32[768,768]{1,0:T(8,128)}), f32[384,768]{1,0:T(8,128)}) %reduce-scatter.19.cloned.1.call-update) | async-done | bytes 1179664 | tf_op jit(solution)/shard_map/reduce_scatter | solution.py:38
  636.1 0.0 all-gather.31.cloned.1.call-start
  636.2 34.1 %reduce-scatter.23.cloned.1.call-done = f32[96,3072]{1,0:T(8,128)} async-done(((f32[192,3072]{1,0:T(8,128)}), f32[96,3072]{1,0:T(8,128)}) %reduce-scatter.23.cloned.1.call-update) | async-done | bytes 1179664 | tf_op jit(solution)/shard_map/reduce_scatter | solution.py:38
  670.3 0.0 all-gather.15.cloned.1.call-start
  670.3 34.6 %all-gather.13.cloned.1.call-done = f32[768,768]{1,0:T(8,128)} async-done(((f32[384,768]{1,0:T(8,128)}), f32[768,768]{1,0:T(8,128)}) %all-gather.13.cloned.1.call-update) | async-done | bytes 2359312 | tf_op jit(solution)/shard_map/all_gather | solution.py:39
  705.0 0.0 all-gather.21.cloned.1.call-start
  705.0 34.5 %all-gather.19.cloned.1.call-done = f32[192,3072]{1,0:T(8,128)} async-done(((f32[96,3072]{1,0:T(8,128)}), f32[192,3072]{1,0:T(8,128)}) %all-gather.19.cloned.1.call-update) | async-done | bytes 2359312 | tf_op jit(solution)/shard_map/all_gather | solution.py:39
  739.5 0.0 all-gather.27.cloned.1.call-start
  739.5 34.6 %all-gather.25.cloned.1.call-done = f32[768,768]{1,0:T(8,128)} async-done(((f32[384,768]{1,0:T(8,128)}), f32[768,768]{1,0:T(8,128)}) %all-gather.25.cloned.1.call-update) | async-done | bytes 2359312 | tf_op jit(solution)/shard_map/all_gather | solution.py:39
  774.2 0.0 all-gather.33.cloned.1.call-start
  774.2 34.5 %all-gather.31.cloned.1.call-done = f32[192,3072]{1,0:T(8,128)} async-done(((f32[96,3072]{1,0:T(8,128)}), f32[192,3072]{1,0:T(8,128)}) %all-gather.31.cloned.1.call-update) | async-done | bytes 2359312 | tf_op jit(solution)/shard_map/all_gather | solution.py:39
  808.7 0.0 all-gather.17.cloned.1.call-start
  808.8 61.7 %all-gather.15.cloned.1.call-done = f32[1536,768]{1,0:T(8,128)} async-done(((f32[768,768]{1,0:T(8,128)}), f32[1536,768]{1,0:T(8,128)}) %all-gather.15.cloned.1.call-update) | async-done | bytes 4718608 | tf_op jit(solution)/shard_map/all_gather | solution.py:40
  870.5 0.0 all-gather.23.cloned.1.call-start
  870.5 61.5 %all-gather.21.cloned.1.call-done = f32[384,3072]{1,0:T(8,128)} async-done(((f32[192,3072]{1,0:T(8,128)}), f32[384,3072]{1,0:T(8,128)}) %all-gather.21.cloned.1.call-update) | async-done | bytes 4718608 | tf_op jit(solution)/shard_map/all_gather | solution.py:40
  932.0 0.0 all-gather.29.cloned.1.call-start
  932.1 61.5 %all-gather.27.cloned.1.call-done = f32[1536,768]{1,0:T(8,128)} async-done(((f32[768,768]{1,0:T(8,128)}), f32[1536,768]{1,0:T(8,128)}) %all-gather.27.cloned.1.call-update) | async-done | bytes 4718608 | tf_op jit(solution)/shard_map/all_gather | solution.py:40
  993.6 0.0 all-gather.35.cloned.1.call-start
  993.7 61.5 %all-gather.33.cloned.1.call-done = f32[384,3072]{1,0:T(8,128)} async-done(((f32[192,3072]{1,0:T(8,128)}), f32[384,3072]{1,0:T(8,128)}) %all-gather.33.cloned.1.call-update) | async-done | bytes 4718608 | tf_op jit(solution)/shard_map/all_gather | solution.py:40
  1055.2 47.7 %add_convert_fusion = bf16[8192,768]{1,0:T(8,128)(2,1)} fusion(bf16[8192,768]{1,0:T(8,128)(2,1)} %add_convert_fusion.1, bf16[8192,3072]{1,0:T(8,128)(2,1)} %fusion.17, bf16[768,3072]{1,0:T(8,128)(2,1)} %param.14), kind=kOutput, calls=%fused_computation.30 | convolution fusion | flops 38673580032 | bytes 80216064 | tf_op jit(solution)/shard_map/dot_general | solution.py:28
  1102.9 18.4 %all-gather.29.cloned.1.call-done = f32[3072,768]{1,0:T(8,128)} async-done(((f32[1536,768]{1,0:T(8,128)}), f32[3072,768]{1,0:T(8,128)}) %all-gather.29.cloned.1.call-update) | async-done | bytes 9437200 | tf_op jit(solution)/shard_map/all_gather | solution.py:41
  1121.3 22.4 %all-gather.35.cloned.1.call-done = f32[768,3072]{1,0:T(8,128)} async-done(((f32[384,3072]{1,0:T(8,128)}), f32[768,3072]{1,0:T(8,128)}) %all-gather.35.cloned.1.call-update) | async-done | bytes 9437200 | tf_op jit(solution)/shard_map/all_gather | solution.py:41
  1143.7 9.3 copy.18
  1153.0 4.8 copy.19
  1157.8 1.5 slice-done.1
  1159.3 0.3 slice-done.2
  1159.6 3.7 copy.20
  1163.3 8.6 copy.21
  (25 shorter events, 0.3 us)
Async XLA Ops:
  7.2 467.0 %reduce-scatter.9.cloned.1.call-start = ((), (), s32[]{:S(2)}) async-start(), calls=%async_computation.12 | async-start | bytes 7077888 | tf_op jit(solution)/shard_map/reduce_scatter | solution.py:37
  74.4 400.3 %reduce-scatter.13.cloned.1.call-start = ((), (), s32[]{:S(2)}) async-start(), calls=%async_computation.17 | async-start | bytes 7077888 | tf_op jit(solution)/shard_map/reduce_scatter | solution.py:37
  212.9 262.5 %reduce-scatter.17.cloned.1.call-start = ((), (), s32[]{:S(2)}) async-start(), calls=%async_computation.22 | async-start | bytes 7077888 | tf_op jit(solution)/shard_map/reduce_scatter | solution.py:37
  335.5 198.5 %reduce-scatter.21.cloned.1.call-start = ((), (), s32[]{:S(2)}) async-start(), calls=%async_computation.27 | async-start | bytes 7077888 | tf_op jit(solution)/shard_map/reduce_scatter | solution.py:37
  474.1 93.8 %reduce-scatter.11.cloned.1.call-start = ((), (), s32[]{:S(2)}) async-start(), calls=%async_computation.13 | async-start | bytes 3538944 | tf_op jit(solution)/shard_map/reduce_scatter | solution.py:38
  474.7 127.2 %reduce-scatter.15.cloned.1.call-start = ((), (), s32[]{:S(2)}) async-start(), calls=%async_computation.18 | async-start | bytes 3538944 | tf_op jit(solution)/shard_map/reduce_scatter | solution.py:38
  475.3 160.8 %reduce-scatter.19.cloned.1.call-start = ((), (), s32[]{:S(2)}) async-start(), calls=%async_computation.23 | async-start | bytes 3538944 | tf_op jit(solution)/shard_map/reduce_scatter | solution.py:38
  476.0 194.2 %reduce-scatter.23.cloned.1.call-start = ((), (), s32[]{:S(2)}) async-start(), calls=%async_computation.28 | async-start | bytes 3538944 | tf_op jit(solution)/shard_map/reduce_scatter | solution.py:38
  534.0 171.0 %all-gather.13.cloned.1.call-start = ((), (), s32[]{:S(2)}) async-start(), calls=%async_computation.14 | async-start | bytes 3538944 | tf_op jit(solution)/shard_map/all_gather | solution.py:39
  567.9 171.5 %all-gather.19.cloned.1.call-start = ((), (), s32[]{:S(2)}) async-start(), calls=%async_computation.19 | async-start | bytes 3538944 | tf_op jit(solution)/shard_map/all_gather | solution.py:39
  602.0 172.2 %all-gather.25.cloned.1.call-start = ((), (), s32[]{:S(2)}) async-start(), calls=%async_computation.24 | async-start | bytes 3538944 | tf_op jit(solution)/shard_map/all_gather | solution.py:39
  636.1 172.6 %all-gather.31.cloned.1.call-start = ((), (), s32[]{:S(2)}) async-start(), calls=%async_computation.29 | async-start | bytes 3538944 | tf_op jit(solution)/shard_map/all_gather | solution.py:39
  670.3 200.2 %all-gather.15.cloned.1.call-start = ((), (), s32[]{:S(2)}) async-start(), calls=%async_computation.15 | async-start | bytes 7077888 | tf_op jit(solution)/shard_map/all_gather | solution.py:40
  705.0 227.0 %all-gather.21.cloned.1.call-start = ((), (), s32[]{:S(2)}) async-start(), calls=%async_computation.20 | async-start | bytes 7077888 | tf_op jit(solution)/shard_map/all_gather | solution.py:40
  739.5 254.1 %all-gather.27.cloned.1.call-start = ((), (), s32[]{:S(2)}) async-start(), calls=%async_computation.25 | async-start | bytes 7077888 | tf_op jit(solution)/shard_map/all_gather | solution.py:40
  774.2 281.0 %all-gather.33.cloned.1.call-start = ((), (), s32[]{:S(2)}) async-start(), calls=%async_computation.30 | async-start | bytes 7077888 | tf_op jit(solution)/shard_map/all_gather | solution.py:40
  808.7 294.2 %all-gather.17.cloned.1.call-start = ((), (), s32[]{:S(2)}) async-start(), calls=%async_computation.16 | async-start | bytes 14155776 | tf_op jit(solution)/shard_map/all_gather | solution.py:41
  870.5 232.5 %all-gather.23.cloned.1.call-start = ((), (), s32[]{:S(2)}) async-start(), calls=%async_computation.21 | async-start | bytes 14155776 | tf_op jit(solution)/shard_map/all_gather | solution.py:41
  932.0 189.3 %all-gather.29.cloned.1.call-start = ((), (), s32[]{:S(2)}) async-start(), calls=%async_computation.26 | async-start | bytes 14155776 | tf_op jit(solution)/shard_map/all_gather | solution.py:41
  993.6 150.1 %all-gather.35.cloned.1.call-start = ((), (), s32[]{:S(2)}) async-start(), calls=%async_computation.31 | async-start | bytes 14155776 | tf_op jit(solution)/shard_map/all_gather | solution.py:41
  1143.7 9.3 copy-start
  1143.7 14.1 %slice-start = ((s8[9437184]{0:T(1024)(128)(4,1)}), s8[4194304]{0:T(1024)(128)(4,1)S(1)}, s32[]{:S(2)}) async-start(s8[9437184]{0:T(1024)(128)(4,1)} %bitcast.23), calls=%async_computation.32 | async-start | bytes 8388608
  1143.7 15.6 %slice-start.1 = ((s8[9437184]{0:T(1024)(128)(4,1)}), s8[4194304]{0:T(1024)(128)(4,1)S(1)}, s32[]{:S(2)}) async-start(s8[9437184]{0:T(1024)(128)(4,1)} %bitcast.23), calls=%async_computation.33 | async-start | bytes 8388608
  1153.0 6.6 slice-start.2
Sparse Core Ops, SparseCore 0:
  74.6 59.6 reduce-scatter.8
  213.0 59.6 reduce-scatter.12
  335.6 59.6 reduce-scatter.16
  474.2 59.6 reduce-scatter.20
  536.0 31.8 reduce-scatter.10
  570.0 31.9 reduce-scatter.14
  604.1 31.9 reduce-scatter.18
  638.3 31.9 reduce-scatter.22
  671.8 33.1 all-gather.12
  706.3 33.1 all-gather.18
  741.0 33.1 all-gather.24
  775.5 33.1 all-gather.30
  810.2 60.1 all-gather.14
  871.8 60.1 all-gather.20
  933.4 60.1 all-gather.26
  994.9 60.1 all-gather.32
  1056.5 19.7 all-gather.16
  1077.8 20.9 all-gather.22
  1100.3 20.9 all-gather.28
  1122.7 20.9 all-gather.34
where the time goes:
time: 1190 us; the launch traced here: 1180 us
  waiting for transfers between devices  621 us (52%)
  matrix products  466 us (39%)
  blocking collectives  35.6 us (3%)
  local copies, waits for them, and re-layouts  28.2 us (2%)
  between operations  14.8 us (1%)
  other arithmetic  12.5 us (1%)
    all_gather x4, waiting for transfers between devices, reduce_grad(): full_sum = lax.all_gather(full_sum, 'second', axis=0, tiled=True)  246 us
    dot_general x2, matrix products, block_backward(): lax.dot_general(grad_y, w_out, CONTRACT_COLS, preferred_element_type=jnp....  157 us
    all_gather x4, waiting for transfers between devices, reduce_grad(): full_sum = lax.all_gather(part_sum, 'third', axis=0, tiled=True)  138 us
    reduce_scatter x4, waiting for transfers between devices, reduce_grad(): lax.psum_scatter(part_sum, 'third', scatter_dimension=0, tiled=True)  136 us
    dot_general x2, matrix products, block_backward(): lax.dot_general(hidden, grad_y, CONTRACT_ROWS, preferred_element_type=jnp...  118 us
    dot_general x2, matrix products, block_backward(): lax.dot_general(x_in, grad_pre, CONTRACT_ROWS, preferred_element_type=jnp...  96.1 us
    dot_general x2, matrix products, block_backward(): lax.dot_general(grad_pre, w_in, CONTRACT_COLS, preferred_element_type=jnp...  95.2 us
    reduce_scatter x4, waiting for transfers between devices, reduce_grad(): lax.psum_scatter(part_sum, 'second', scatter_dimension=0, tiled=True)  57.9 us
  transfers between devices with their start and end apart: 20, of which 15 were waited for; matrix products, arithmetic and copies ran while one was open for 36% of the time, Pallas kernels for 0%

commit v1 on v0

--- a/solution.py
+++ b/solution.py
@@ -29,16 +29,57 @@
     return w_out_grad, w_in_grad, grad_x
 
 
-def reduce_grad(grad, group_size):
+def reduce_whole(grad):
+    return lax.psum(grad.astype(jnp.float32), AXES)
+
+
+def reduce_scattered(grad):
+    part = lax.psum_scatter(grad.astype(jnp.float32), AXES, scatter_dimension=0, tiled=True)
+    return lax.all_gather(part, AXES, axis=0, tiled=True)
+
+
+def pair_half(grad, group_size):
     row_count, col_count = grad.shape
-    pieces = grad.reshape(group_size, row_count // group_size, col_count)
-    received = lax.all_to_all(pieces, 'group', 0, 0)
-    part_sum = jnp.sum(received, axis=0, dtype=jnp.float32)
-    part_sum = lax.psum_scatter(part_sum, 'second', scatter_dimension=0, tiled=True)
-    part_sum = lax.psum_scatter(part_sum, 'third', scatter_dimension=0, tiled=True)
-    full_sum = lax.all_gather(part_sum, 'third', axis=0, tiled=True)
-    full_sum = lax.all_gather(full_sum, 'second', axis=0, tiled=True)
-    return lax.all_gather(full_sum, 'group', axis=0, tiled=True)
+    half = row_count // group_size
+    core = lax.axis_index('group')
+    send = lax.dynamic_slice_in_dim(grad, (1 - core) * half, half)
+    keep = lax.dynamic_slice_in_dim(grad, core * half, half)
+    received = lax.ppermute(send, 'group', [(0, 1), (1, 0)])
+    return keep.astype(jnp.float32) + received.astype(jnp.float32)
+
+
+def pair_join(part):
+    received = lax.ppermute(part, 'group', [(0, 1), (1, 0)])
+    core = lax.axis_index('group')
+    return jnp.concatenate([jnp.where(core == 0, part, received), jnp.where(core == 0, received, part)], axis=0)
+
+
+def reduce_chips(grad, group_size):
+    part = lax.psum(pair_half(grad, group_size), ('third', 'second'))
+    return pair_join(part)
+
+
+def swap(part, axis):
+    return lax.ppermute(part, axis, [(0, 1), (1, 0)])
+
+
+def swap_sum(part, first, second):
+    half = part.shape[0] // 2
+    pos = lax.axis_index(first)
+    send = lax.dynamic_slice_in_dim(part, (1 - pos) * half, half)
+    keep = lax.dynamic_slice_in_dim(part, pos * half, half)
+    mine = keep + swap(send, first)
+    mine = mine + swap(mine, second)
+    other = swap(mine, first)
+    return jnp.concatenate([jnp.where(pos == 0, mine, other), jnp.where(pos == 0, other, mine)], axis=0)
+
+
+def reduce_swaps(grad, group_size):
+    part = pair_half(grad, group_size)
+    half = part.shape[0] // 2
+    low = swap_sum(part[:half], 'second', 'third')
+    high = swap_sum(part[half:], 'third', 'second')
+    return pair_join(jnp.concatenate([low, high], axis=0))
 
 
 def solution(mesh):
@@ -46,11 +87,11 @@
 
     def device_step(x_one, z_one, x_two, z_two, grad_out, w1_in, w1_out, w2_in, w2_out):
         w2o_grad, w2i_grad, dx_two = block_backward(x_two, z_two, grad_out, w2_in, w2_out)
-        sum_w2o = reduce_grad(w2o_grad, group_size)
-        sum_w2i = reduce_grad(w2i_grad, group_size)
+        sum_w2o = reduce_whole(w2o_grad)
+        sum_w2i = reduce_chips(w2i_grad, group_size)
         w1o_grad, w1i_grad, dx_one = block_backward(x_one, z_one, dx_two, w1_in, w1_out)
-        sum_w1o = reduce_grad(w1o_grad, group_size)
-        sum_w1i = reduce_grad(w1i_grad, group_size)
+        sum_w1o = reduce_swaps(w1o_grad, group_size)
+        sum_w1i = reduce_scattered(w1i_grad)
         return sum_w2o, sum_w2i, sum_w1o, sum_w1i, dx_one
 
     row_spec = P(AXES, None)

time: 1190 us -> 712 us (0.60)
  waiting for transfers between devices: 621 us -> 151 us
  blocking collectives: 35.6 us -> 0 us
  other arithmetic: 12.5 us -> 33.8 us
    all_gather x12 -> x1, waiting for transfers between devices: 425 us -> 0.01 us  [reduce_scattered(): return lax.all_gather(part, AXES, axis=0, tiled=True)]
    reduce_scatter x8 -> x1, waiting for transfers between devices: 194 us -> 10.9 us  [reduce_scattered(): lax.psum_scatter(grad.astype(jnp.float32), AXES, scatter_dimension=0, til...]
    ppermute x0 -> x10, waiting for transfers between devices: none -> 94.7 us  [the longest x6 86.1 us: swap(): return lax.ppermute(part, axis, [(0, 1), (1, 0)])]
    psum x0 -> x2, waiting for transfers between devices: none -> 45.5 us  [the longest x1 45.5 us: reduce_whole(): return lax.psum(grad.astype(jnp.float32), AXES)]
    all_to_all x4 -> x0, blocking collectives: 35.6 us -> none  [reduce_grad(): received = lax.all_to_all(pieces, 'group', 0, 0)]
    reduce_sum x4 -> x0, other arithmetic: 12.5 us -> none  [reduce_grad(): part_sum = jnp.sum(received, axis=0, dtype=jnp.float32)]
    unnamed x12 -> x24, local copies, waits for them, and re-layouts: 28.2 us -> 35.4 us
  transfers between devices with their start and end apart: 20 -> 14, of which waited for: 15 -> 7; matrix products, arithmetic and copies ran while one was open for 36% -> 37% of each run, Pallas kernels for 0% -> 0%
where the time goes in v1:
time: 712 us; the launch traced here: 703 us
  matrix products  457 us (64%)
  waiting for transfers between devices  151 us (21%)
  local copies, waits for them, and re-layouts  38.9 us (5%)
  other arithmetic  33.8 us (5%)
  between operations  16.1 us (2%)
    dot_general x2, matrix products, block_backward(): lax.dot_general(grad_y, w_out, CONTRACT_COLS, preferred_element_type=jnp....  150 us
    dot_general x2, matrix products, block_backward(): lax.dot_general(hidden, grad_y, CONTRACT_ROWS, preferred_element_type=jnp...  119 us
    dot_general x2, matrix products, block_backward(): lax.dot_general(grad_pre, w_in, CONTRACT_COLS, preferred_element_type=jnp...  94.6 us
    dot_general x2, matrix products, block_backward(): lax.dot_general(x_in, grad_pre, CONTRACT_ROWS, preferred_element_type=jnp...  92.7 us
    ppermute x6, waiting for transfers between devices, swap(): return lax.ppermute(part, axis, [(0, 1), (1, 0)])  86.1 us
    psum x1, waiting for transfers between devices, reduce_whole(): return lax.psum(grad.astype(jnp.float32), AXES)  45.5 us
    unnamed x24, local copies, waits for them, and re-layouts  35.4 us
  transfers between devices with their start and end apart: 14, of which 7 were waited for; matrix products, arithmetic and copies ran while one was open for 37% of the time, Pallas kernels for 0%

profile of v1, /device:TPU:0, one launch (start us, length us, event | category | flops | bytes accessed | tf_op | source)
XLA Modules:
  0.0 703.5 jit_solution(3576808025594836946)
XLA Ops:
  8.0 0.0 reduce-scatter.4.cloned.1.call-start
  8.1 78.4 %fusion.8 = bf16[8192,3072]{1,0:T(8,128)(2,1)} fusion(bf16[8192,3072]{1,0:T(8,128)(2,1)} %param.12, bf16[8192,768]{1,0:T(8,128)(2,1)} %param.13, bf16[3072,768]{1,0:T(8,128)(2,1)} %param.17), kind=kOutput, calls=%fused_computation.18 | convolution fusion | flops 38931529728 | bytes 117964800 | tf_op jit(solution)/shard_map/dot_general | solution.py:25
  86.5 46.9 %add_convert_fusion.1 = bf16[8192,768]{1,0:T(8,128)(2,1)} fusion(bf16[8192,768]{1,0:T(8,128)(2,1)} %param.13, bf16[8192,3072]{1,0:T(8,128)(2,1)} %fusion.8, bf16[768,3072]{1,0:T(8,128)(2,1)S(1)} %copy-done.8), kind=kOutput, calls=%fused_computation.31 | convolution fusion | flops 38673580032 | bytes 80216064 | tf_op jit(solution)/shard_map/dot_general | solution.py:28
  133.4 71.8 %fusion.17 = bf16[8192,3072]{1,0:T(8,128)(2,1)} fusion(bf16[8192,3072]{1,0:T(8,128)(2,1)} %param.10, bf16[8192,768]{1,0:T(8,128)(2,1)} %add_convert_fusion.1, bf16[3072,768]{1,0:T(8,128)(2,1)S(1)} %copy-done.9), kind=kOutput, calls=%fused_computation.27 | convolution fusion | flops 38931529728 | bytes 117964800 | tf_op jit(solution)/shard_map/dot_general | solution.py:25
  205.1 45.3 %convert_bitcast_fusion = f32[768,3072]{0,1:T(8,128)} fusion(bf16[8192,3072]{1,0:T(8,128)(2,1)} %fusion.17, bf16[8192,768]{1,0:T(8,128)(2,1)S(1)} %copy-done.7), kind=kOutput, calls=%fused_computation.34 | convolution fusion | flops 38659424256 | bytes 72351744 | tf_op jit(solution)/shard_map/dot_general | solution.py:27
  250.5 9.6 %copy.18 = f32[768,3072]{1,0:T(8,128)} copy(f32[768,3072]{0,1:T(8,128)} %convert_bitcast_fusion) | data formatting | bytes 18874368
  260.1 0.0 reduce-scatter.4.cloned.1.call-update
  260.1 0.0 all-reduce.5.cloned.1.call-start
  260.2 47.4 %convolution_convert_fusion.1 = bf16[3072,768]{1,0:T(8,128)(2,1)S(1)} fusion(bf16[8192,3072]{1,0:T(8,128)(2,1)} %fusion.8, bf16[8192,768]{1,0:T(8,128)(2,1)} %param.11), kind=kOutput, calls=%fused_computation.39 | convolution fusion | flops 38657064960 | bytes 67633152 | tf_op jit(solution)/shard_map/dot_general | solution.py:27
  307.6 0.0 copy-start.6
  307.6 2.2 copy-done.6
  309.7 0.2 dynamic-slice_bitcast_fusion
  310.0 0.9 collective-permute-start
  310.9 4.2 collective-permute-done
  315.0 5.0 bitcast_add_fusion
  320.0 0.0 all-reduce.5.cloned.1.call-update
  320.1 0.0 all-gather.2.cloned.1.call-start
  320.1 10.9 %reduce-scatter.4.cloned.1.call-done = f32[96,3072]{1,0:T(8,128)} async-done(((f32[768,3072]{1,0:T(8,128)}), f32[96,3072]{1,0:T(8,128)}) %reduce-scatter.4.cloned.1.call-update) | async-done | bytes 1179664 | tf_op jit(solution)/shard_map/reduce_scatter | solution.py:37
  331.0 0.0 all-gather.2.cloned.1.call-update
  331.1 0.0 all-reduce.3.cloned.1.call-start
  331.1 64.3 %fusion.28 = bf16[3072,768]{1,0:T(8,128)(2,1)} fusion(bf16[8192,768]{1,0:T(8,128)(2,1)} %add_convert_fusion.1, bf16[8192,3072]{1,0:T(8,128)(2,1)} %param.10), kind=kOutput, calls=%fused_computation.37 | convolution fusion | flops 38808059904 | bytes 67633152 | tf_op jit(solution)/shard_map/dot_general | solution.py:24
  395.4 1.8 constant_dynamic-slice_fusion.2
  397.2 0.0 collective-permute-start.2
  397.2 4.5 collective-permute-done.2
  401.7 2.9 convert_add_fusion
  404.6 0.3 fusion.33
  404.9 0.0 copy-start.5
  404.9 1.4 copy-done.5
  406.3 0.1 constant_dynamic-slice_fusion.1
  406.4 1.5 collective-permute-start.3
  407.9 1.1 constant_dynamic-slice_fusion
  409.0 0.6 collective-permute-start.6
  409.5 39.1 %collective-permute-done.3 = f32[384,768]{1,0:T(8,128)} collective-permute-done((f32[384,768]{1,0:T(8,128)S(1)}, f32[384,768]{1,0:T(8,128)}, u32[]{:S(2)}, u32[]{:S(2)}) %collective-permute-start.3) | collective-permute-done | bytes 1179680 | tf_op jit(solution)/shard_map/ppermute | solution.py:63
  448.6 1.8 dynamic-slice_add_fusion.1
  450.4 1.2 collective-permute-start.4
  451.6 2.3 collective-permute-done.6
  453.9 1.4 dynamic-slice_add_fusion
  455.3 0.0 collective-permute-start.7
  455.3 44.6 %collective-permute-done.4 = f32[384,768]{1,0:T(8,128)S(1)} collective-permute-done((f32[384,768]{1,0:T(8,128)S(1)}, f32[384,768]{1,0:T(8,128)S(1)}, u32[]{:S(2)}, u32[]{:S(2)}) %collective-permute-start.4) | collective-permute-done | bytes 1179680 | tf_op jit(solution)/shard_map/ppermute | solution.py:63
  499.9 0.1 add.79
  500.1 0.6 collective-permute-start.5
  500.7 0.0 collective-permute-done.7
  500.7 0.1 add.83
  500.8 1.5 collective-permute-start.8
  502.3 54.8 %fusion.25 = f32[3072,768]{1,0:T(8,128)} fusion(bf16[8192,768]{1,0:T(8,128)(2,1)} %param.13, bf16[8192,3072]{1,0:T(8,128)(2,1)} %param.12), kind=kOutput, calls=%fused_computation.36 | convolution fusion | flops 38810419200 | bytes 72351744 | tf_op jit(solution)/shard_map/dot_general | solution.py:24
  557.1 0.0 all-reduce.3.cloned.1.call-update
  557.1 0.0 collective-permute-done.5
  557.2 0.2 broadcast_select_fusion.7
  557.3 0.0 collective-permute-done.8
  557.4 2.3 broadcast_select_fusion.5
  559.6 0.0 copy-start.3
  559.7 2.7 pad_maximum_fusion.2
  562.4 0.2 copy-done.3
  562.6 0.0 collective-permute-start.9
  562.6 0.5 collective-permute-start.1
  563.1 47.7 %add_convert_fusion = bf16[8192,768]{1,0:T(8,128)(2,1)} fusion(bf16[8192,768]{1,0:T(8,128)(2,1)} %add_convert_fusion.1, bf16[8192,3072]{1,0:T(8,128)(2,1)} %fusion.17, bf16[768,3072]{1,0:T(8,128)(2,1)} %param.14), kind=kOutput, calls=%fused_computation.30 | convolution fusion | flops 38673580032 | bytes 80216064 | tf_op jit(solution)/shard_map/dot_general | solution.py:28
  610.8 4.1 broadcast_select_fusion.1
  614.9 4.3 pad_maximum_fusion.1
  619.2 4.4 broadcast_select_fusion.3
  623.6 4.5 pad_maximum_fusion
  628.1 9.6 %copy.17 = f32[768,3072]{1,0:T(8,128)} copy(f32[768,3072]{0,1:T(8,128)} %pad_maximum_fusion) | data formatting | bytes 18874368
  637.7 45.5 %all-reduce.3.cloned.1.call-done = f32[3072,768]{1,0:T(8,128)} async-done(((f32[3072,768]{1,0:T(8,128)}), f32[3072,768]{1,0:T(8,128)}) %all-reduce.3.cloned.1.call-update) | async-done | bytes 9437200 | tf_op jit(solution)/shard_map/psum | solution.py:33
  683.2 8.7 %copy.23 = f32[3072,768]{1,0:T(8,128)} copy(f32[3072,768]{1,0:T(8,128)} %all-reduce.3.cloned.1.call-done) | data formatting | bytes 18874368
  691.9 3.7 copy.24
  (18 shorter events, 0.0 us)
Async XLA Ops:
  8.0 323.0 %reduce-scatter.4.cloned.1.call-start = ((), (), s32[]{:S(2)}) async-start(), calls=%async_computation.4 | async-start | bytes 10616832 | tf_op jit(solution)/shard_map/reduce_scatter | solution.py:37
  8.0 78.4 %copy-start.8 = (bf16[768,3072]{1,0:T(8,128)(2,1)S(1)}, bf16[768,3072]{1,0:T(8,128)(2,1)}, u32[]{:S(2)}) copy-start(bf16[768,3072]{1,0:T(8,128)(2,1)} %param.16) | copy-start | bytes 14155780
  86.5 46.9 %copy-start.9 = (bf16[3072,768]{1,0:T(8,128)(2,1)S(1)}, bf16[3072,768]{1,0:T(8,128)(2,1)}, u32[]{:S(2)}) copy-start(bf16[3072,768]{1,0:T(8,128)(2,1)} %param.15) | copy-start | bytes 14155780
  133.4 71.8 %copy-start.7 = (bf16[8192,768]{1,0:T(8,128)(2,1)S(1)}, bf16[8192,768]{1,0:T(8,128)(2,1)}, u32[]{:S(2)}) copy-start(bf16[8192,768]{1,0:T(8,128)(2,1)} %param.9) | copy-start | bytes 37748740
  260.1 302.5 %all-reduce.5.cloned.1.call-start = ((), (), s32[]{:S(2)}) async-start(), calls=%async_computation.2 | async-start | bytes 9437184 | tf_op jit(solution)/shard_map/psum | solution.py:58
  307.6 2.2 copy-start.6
  310.0 5.0 collective-permute-start
  320.1 317.6 %all-gather.2.cloned.1.call-start = ((), (), s32[]{:S(2)}) async-start(), calls=%async_computation.3 | async-start | bytes 10616832 | tf_op jit(solution)/shard_map/all_gather | solution.py:38
  331.1 352.1 %all-reduce.3.cloned.1.call-start = ((), (), s32[]{:S(2)}) async-start(), calls=%async_computation.1 | async-start | bytes 18874368 | tf_op jit(solution)/shard_map/psum | solution.py:33
  397.2 4.5 collective-permute-start.2
  404.9 1.4 copy-start.5
  406.4 42.3 %collective-permute-start.3 = (f32[384,768]{1,0:T(8,128)S(1)}, f32[384,768]{1,0:T(8,128)}, u32[]{:S(2)}, u32[]{:S(2)}) collective-permute-start(f32[384,768]{1,0:T(8,128)S(1)} %constant_dynamic-slice_fusion.1), channel_id=1, source_target_pairs={{0,2},{2,0},{1,3},{3,1},{4,6},{6,4},{5,7},{7,5}} | collective-permute-start | bytes 3538952 | tf_op jit(solution)/shard_map/ppermute | solution.py:63
  409.0 44.9 %collective-permute-start.6 = (f32[384,768]{1,0:T(8,128)}, f32[384,768]{1,0:T(8,128)}, u32[]{:S(2)}, u32[]{:S(2)}) collective-permute-start(f32[384,768]{1,0:T(8,128)} %constant_dynamic-slice_fusion), channel_id=1, source_target_pairs={{0,4},{4,0},{1,5},{5,1},{2,6},{6,2},{3,7},{7,3}} | collective-permute-start | bytes 3538952 | tf_op jit(solution)/shard_map/ppermute | solution.py:63
  450.4 49.5 %collective-permute-start.4 = (f32[384,768]{1,0:T(8,128)S(1)}, f32[384,768]{1,0:T(8,128)S(1)}, u32[]{:S(2)}, u32[]{:S(2)}) collective-permute-start(f32[384,768]{1,0:T(8,128)S(1)} %dynamic-slice_add_fusion.1), channel_id=1, source_target_pairs={{0,4},{4,0},{1,5},{5,1},{2,6},{6,2},{3,7},{7,3}} | collective-permute-start | bytes 3538952 | tf_op jit(solution)/shard_map/ppermute | solution.py:63
  455.3 45.4 %collective-permute-start.7 = (f32[384,768]{1,0:T(8,128)S(1)}, f32[384,768]{1,0:T(8,128)S(1)}, u32[]{:S(2)}, u32[]{:S(2)}) collective-permute-start(f32[384,768]{1,0:T(8,128)S(1)} %dynamic-slice_add_fusion), channel_id=1, source_target_pairs={{0,2},{2,0},{1,3},{3,1},{4,6},{6,4},{5,7},{7,5}} | collective-permute-start | bytes 3538952 | tf_op jit(solution)/shard_map/ppermute | solution.py:63
  500.1 57.1 %collective-permute-start.5 = (f32[384,768]{1,0:T(8,128)S(1)}, f32[384,768]{1,0:T(8,128)S(1)}, u32[]{:S(2)}, u32[]{:S(2)}) collective-permute-start(f32[384,768]{1,0:T(8,128)S(1)} %add.79), channel_id=1, source_target_pairs={{0,2},{2,0},{1,3},{3,1},{4,6},{6,4},{5,7},{7,5}} | collective-permute-start | bytes 3538952 | tf_op jit(solution)/shard_map/ppermute | solution.py:63
  500.8 56.5 %collective-permute-start.8 = (f32[384,768]{1,0:T(8,128)S(1)}, f32[384,768]{1,0:T(8,128)}, u32[]{:S(2)}, u32[]{:S(2)}) collective-permute-start(f32[384,768]{1,0:T(8,128)S(1)} %add.83), channel_id=1, source_target_pairs={{0,4},{4,0},{1,5},{5,1},{2,6},{6,2},{3,7},{7,3}} | collective-permute-start | bytes 3538952 | tf_op jit(solution)/shard_map/ppermute | solution.py:63
  557.3 2.3 copy-start
  557.3 5.0 copy-start.1
  559.6 2.7 copy-start.2
  559.6 2.9 copy-start.3
  562.6 48.2 %collective-permute-start.9 = (f32[1536,768]{1,0:T(8,128)}, f32[1536,768]{1,0:T(8,128)}, u32[]{:S(2)}, u32[]{:S(2)}) collective-permute-start(f32[1536,768]{1,0:T(8,128)} %pad_maximum_fusion.2), channel_id=1, source_target_pairs={{0,1},{1,0},{2,3},{3,2},{4,5},{5,4},{6,7},{7,6}} | collective-permute-start | bytes 14155784 | tf_op jit(solution)/shard_map/ppermute | solution.py:52
  562.6 56.6 %collective-permute-start.1 = (f32[384,3072]{0,1:T(8,128)}, f32[384,3072]{0,1:T(8,128)}, u32[]{:S(2)}, u32[]{:S(2)}) collective-permute-start(f32[384,3072]{0,1:T(8,128)} %all-reduce.5.cloned.1.call-done), channel_id=1, source_target_pairs={{0,1},{1,0},{2,3},{3,2},{4,5},{5,4},{6,7},{7,6}} | collective-permute-start | bytes 14155784 | tf_op jit(solution)/shard_map/ppermute | solution.py:52
  683.2 8.7 %copy-start.4 = (f32[768,3072]{1,0:T(8,128)S(1)}, f32[768,3072]{1,0:T(8,128)}, u32[]{:S(2)}) copy-start(f32[768,3072]{1,0:T(8,128)} %all-gather.2.cloned.1.call-done) | copy-start | bytes 28311556
Sparse Core Ops, SparseCore 0:
  260.2 70.7 reduce-scatter.3
  332.8 63.9 all-gather.1
Sparse Core Ops, SparseCore 1:
  320.1 177.0 all-reduce.4
  557.2 125.9 all-reduce.2

commit v2 on v0

v2 whole, which is shorter than its diff:
```python
import functools
import math
import jax
import jax.numpy as jnp
from jax import lax
from jax.experimental import pallas as pl
from jax.experimental.pallas import tpu as pltpu
from jax.sharding import PartitionSpec as P

AXES = ('third', 'second', 'group')
INV_ROOT_TWO = math.sqrt(0.5)
INV_ROOT_TWO_PI = 1.0 / math.sqrt(2.0 * math.pi)
CONTRACT_ROWS = (((0,), (0,)), ((), ()))
CONTRACT_COLS = (((1,), (1,)), ((), ()))
TM = 512
VMEM_LIMIT = 60 * 1024 * 1024
MESH = pl.DeviceIdType.MESH
HALVES = 2
ANY = pl.BlockSpec(memory_space=pl.ANY)


def dot(lhs, rhs, dims):
    return lax.dot_general(lhs, rhs, dims, preferred_element_type=jnp.float32)


def gelu_pair(z_pre):
    z_val = z_pre.astype(jnp.float32)
    cdf_val = 0.5 * (1.0 + lax.erf(z_val * INV_ROOT_TWO))
    hidden = (z_val * cdf_val).astype(jnp.bfloat16)
    slope = cdf_val + z_val * jnp.exp(-0.5 * z_val * z_val) * INV_ROOT_TWO_PI
    return hidden, slope


class Lane:
    def __init__(self, keep, send, prior, own, other, recv_pair, cur, recv_one, mid, recv_two, fin, send_sem, recv_sem, copy_sem):
        self.keep, self.send, self.prior, self.own, self.other = keep, send, prior, own, other
        self.recv_pair, self.cur, self.recv_one, self.mid, self.recv_two, self.fin = recv_pair, cur, recv_one, mid, recv_two, fin
        self.send_sem, self.recv_sem, self.copy_sem = send_sem, recv_sem, copy_sem
        self.rows = cur.shape[1]
        self.half = self.rows // HALVES
        self.pos = (lax.axis_index('second'), lax.axis_index('third'))
        self.near = ({'second': 1 - self.pos[0]}, {'third': 1 - self.pos[1]})
        self.pair = {'group': 1 - lax.axis_index('group')}

    def remote(self, src, dst, slot, device):
        return pltpu.make_async_remote_copy(
            src_ref=src,
            dst_ref=dst,
            send_sem=self.send_sem.at[slot],
            recv_sem=self.recv_sem.at[slot],
            device_id=device,
            device_id_type=MESH,
        )

    def part(self, half):
        return pl.ds(half * self.half, self.half)

    def mine(self, side):
        return 2 * side + self.pos[side]

    def exchange(self):
        return self.remote(self.send, self.recv_pair, 0, self.pair)

    def join(self):
        return self.remote(self.prior, self.other, 1, self.pair)

    def scatter(self, side, half):
        src = self.cur.at[2 * side + 1 - self.pos[side], self.part(half)]
        return self.remote(src, self.recv_one.at[side, self.part(half)], 2 + 2 * side + half, self.near[side])

    def swap(self, side, half):
        src = self.mid.at[side, self.part(half)]
        return self.remote(src, self.recv_two.at[side, self.part(half)], 6 + 2 * side + half, self.near[1 - side])

    def gather(self, side, half):
        place = self.fin.at[self.mine(side), self.part(half)]
        return self.remote(place, place, 10 + 2 * side + half, self.near[side])

    def gathered(self, side, half):
        place = self.fin.at[2 * side + 1 - self.pos[side], self.part(half)]
        return self.remote(place, place, 10 + 2 * side + half, self.near[side])

    def enter(self):
        barrier = pltpu.get_barrier_semaphore()
        for device in (self.pair, *self.near):
            pl.semaphore_signal(barrier, inc=1, device_id=device, device_id_type=MESH)
        pl.semaphore_wait(barrier, 3)
        self.exchange().start()
        if self.prior is not None:
            self.join().start()

    def add_pair(self):
        self.exchange().wait_recv()
        for quarter in range(4):
            rows = pl.ds(quarter * self.rows, self.rows)
            self.cur[quarter] = self.keep[rows, :].astype(jnp.float32) + self.recv_pair[rows, :].astype(jnp.float32)
        for half in range(HALVES):
            for side in range(2):
                self.scatter(side, half).start()

    def add_first(self, half):
        for side in range(2):
            self.scatter(side, half).wait_recv()
            rows = self.part(half)
            self.mid[side, rows, :] = self.cur[self.mine(side), rows, :] + self.recv_one[side, rows, :]
            self.swap(side, half).start()

    def add_second(self, half):
        for side in range(2):
            self.swap(side, half).wait_recv()
            rows = self.part(half)
            self.fin[self.mine(side), rows, :] = self.mid[side, rows, :] + self.recv_two[side, rows, :]
            self.gather(side, half).start()

    def leave(self):
        for half in range(HALVES):
            for side in range(2):
                self.gathered(side, half).wait_recv()
        out = pltpu.make_async_copy(self.fin, self.own, self.copy_sem)
        out.start()
        self.exchange().wait_send()
        if self.prior is not None:
            self.join().wait()
        for half in range(HALVES):
            for side in range(2):
                self.scatter(side, half).wait_send()
                self.swap(side, half).wait_send()
                self.gather(side, half).wait_send()
        out.wait()

    def before(self, step):
        pl.when(step == 0)(self.enter)
        pl.when(step == 2)(self.add_pair)
        pl.when(step == 5)(lambda: self.add_first(0))
        pl.when(step == 8)(lambda: self.add_first(1))
        pl.when(step == 10)(lambda: self.add_second(0))
        pl.when(step == 12)(lambda: self.add_second(1))

    def after(self, step):
        pl.when(step == pl.num_programs(0) - 1)(self.leave)


def lane_specs(load, width):
    if load is None:
        return [], [], [], [], []
    keep, send, prior = load
    quarter = (width // 4, width)
    operands = [keep, send] + ([] if prior is None else [prior])
    in_specs = [pl.BlockSpec((width, width), lambda i, *_: (0, 0))] + [ANY] * (len(operands) - 1)
    whole = jax.ShapeDtypeStruct((4, *quarter), jnp.float32)
    outs = [whole] * (1 if prior is None else 2)
    scratch = [
        pltpu.VMEM((width, width), jnp.bfloat16),
        pltpu.VMEM((4, *quarter), jnp.float32),
        pltpu.VMEM((2, *quarter), jnp.float32),
        pltpu.VMEM((2, *quarter), jnp.float32),
        pltpu.VMEM((2, *quarter), jnp.float32),
        pltpu.VMEM((4, *quarter), jnp.float32),
        pltpu.SemaphoreType.DMA((14,)),
        pltpu.SemaphoreType.DMA((14,)),
        pltpu.SemaphoreType.DMA,
    ]
    return operands, in_specs, outs, [ANY] * len(outs), scratch


def split_lane(mode, refs, n_in, n_out):
    extra_in, extra_out = {'none': (0, 0), 'first': (2, 1), 'next': (3, 2)}[mode]
    refs = list(refs)
    ins, refs = refs[:n_in], refs[n_in:]
    lane_in, refs = refs[:extra_in], refs[extra_in:]
    outs, refs = refs[:n_out], refs[n_out:]
    lane_out, refs = refs[:extra_out], refs[extra_out:]
    lane = None
    if mode != 'none':
        lane_scratch, refs = refs[:9], refs[9:]
        if mode == 'first':
            lane_in, lane_out = [*lane_in, None], [*lane_out, None]
        lane = Lane(*lane_in, *lane_out, *lane_scratch)
    return ins, outs, refs, lane


def lane_mode(load):
    return 'none' if load is None else 'first' if load[2] is None else 'next'


def params(load, ident):
    extra = {} if load is None else dict(collective_id=ident, has_side_effects=True)
    return pltpu.CompilerParams(dimension_semantics=('arbitrary',), vmem_limit_bytes=VMEM_LIMIT, **extra)


def chunk_kernel(mode, *refs):
    ins, outs, scratch, lane = split_lane(mode, refs, 4, 3)
    z_ref, dy_ref, x_ref, w_ref = ins
    dz_ref, keep_ref, send_ref = outs
    acc_o, acc_i, turned = scratch
    step = pl.program_id(0)
    if lane is not None:
        lane.before(step)

    @pl.when(step == 0)
    def _():
        acc_o[...] = jnp.zeros_like(acc_o)
        acc_i[...] = jnp.zeros_like(acc_i)
        turned[...] = w_ref[...].T

    hidden, slope = gelu_pair(z_ref[...])
    dz = (jnp.dot(dy_ref[...], turned[...], preferred_element_type=jnp.float32) * slope).astype(jnp.bfloat16)
    dz_ref[...] = dz
    acc_o[...] += dot(hidden, dy_ref[...], CONTRACT_ROWS)
    acc_i[...] += dot(x_ref[...], dz, CONTRACT_ROWS)

    @pl.when(step == pl.num_programs(0) - 1)
    def _():
        first = lax.axis_index('group') == 0

        @pl.when(first)
        def _():
            keep_ref[...] = acc_o[...].astype(jnp.bfloat16)
            send_ref[...] = acc_i[...].astype(jnp.bfloat16)

        @pl.when(jnp.logical_not(first))
        def _():
            keep_ref[...] = acc_i[...].astype(jnp.bfloat16)
            send_ref[...] = acc_o[...].astype(jnp.bfloat16)

    if lane is not None:
        lane.after(step)


def chunk_grads(z_pre, grad_y, x_in, w_out, part, load, ident):
    tokens, width = grad_y.shape
    square = pl.BlockSpec((width, width), lambda i: (0, 0))
    rows = pl.BlockSpec((TM, width), lambda i: (i, 0))
    operands, in_specs, outs, out_specs, scratch = lane_specs(load, width)
    flops = 6 * tokens * width * width
    return pl.pallas_call(
        functools.partial(chunk_kernel, lane_mode(load)),
        out_shape=[
            jax.ShapeDtypeStruct((tokens, width), jnp.bfloat16),
            jax.ShapeDtypeStruct((width, width), jnp.bfloat16),
            jax.ShapeDtypeStruct((width, width), jnp.bfloat16),
            *outs,
        ],
        grid=(tokens // TM,),
        in_specs=[
            pl.BlockSpec((TM, width), lambda i: (i, part)),
            rows,
            rows,
            pl.BlockSpec((width, width), lambda i: (part, 0)),
            *in_specs,
        ],
        out_specs=[rows, square, square, *out_specs],
        scratch_shapes=[
            *scratch,
            pltpu.VMEM((width, width), jnp.float32),
            pltpu.VMEM((width, width), jnp.float32),
            pltpu.VMEM((width, width), jnp.bfloat16),
        ],
        compiler_params=params(load, ident),
        cost_estimate=pl.CostEstimate(flops=flops, bytes_accessed=8 * tokens * width, transcendentals=2 * tokens * width),
        name='chunk_grads',
    )(z_pre, grad_y, x_in, w_out, *operands)


def input_kernel(mode, count, *refs):
    ins, outs, scratch, lane = split_lane(mode, refs, 2 + count, 1)
    dy_ref, *dz_refs, w_ref = ins
    (turned,) = scratch
    step = pl.program_id(0)
    if lane is not None:
        lane.before(step)

    @pl.when(step == 0)
    def _():
        turned[...] = w_ref[...].T

    total = dy_ref[...].astype(jnp.float32)
    dz = jnp.concatenate([ref[...] for ref in dz_refs], axis=1)
    total = total + jnp.dot(dz, turned[...], preferred_element_type=jnp.float32)
    outs[0][...] = total.astype(jnp.bfloat16)
    if lane is not None:
        lane.after(step)


def input_grad(grad_y, dz_parts, w_in, load, ident):
    tokens, width = grad_y.shape
    rows = pl.BlockSpec((TM, width), lambda i: (i, 0))
    operands, in_specs, outs, out_specs, scratch = lane_specs(load, width)
    return pl.pallas_call(
        functools.partial(input_kernel, lane_mode(load), len(dz_parts)),
        out_shape=[jax.ShapeDtypeStruct((tokens, width), jnp.bfloat16), *outs],
        grid=(tokens // TM,),
        in_specs=[rows] * (1 + len(dz_parts)) + [pl.BlockSpec(w_in.shape, lambda i: (0, 0)), *in_specs],
        out_specs=[rows, *out_specs],
        scratch_shapes=[*scratch, pltpu.VMEM(w_in.shape[::-1], jnp.bfloat16)],
        compiler_params=params(load, ident),
        cost_estimate=pl.CostEstimate(flops=2 * tokens * width * w_in.shape[1], bytes_accessed=12 * tokens * width, transcendentals=0),
        name='input_grad',
    )(grad_y, *dz_parts, w_in, *operands)


def place_kernel(core_ref, *refs):
    count = (len(refs) - 5) // 2
    owns, others = refs[:count], refs[count:2 * count]
    sum_out, sum_in, held, in_sem, out_sem = refs[2 * count:]
    width = sum_in.shape[0]
    quarter = width // 4
    first = core_ref[0] == 0

    def load(slot):
        return pltpu.make_async_copy((*owns, *others)[slot], held.at[slot], in_sem.at[slot])

    def store(slot, into_out, quad):
        part = slot % count
        if into_out:
            dst = sum_out.at[pl.ds(part * width + quad * quarter, quarter), :]
        else:
            dst = sum_in.at[pl.ds(quad * quarter, quarter), pl.ds(part * width, width)]
        return pltpu.make_async_copy(held.at[slot, quad], dst, out_sem.at[slot, quad])

    for slot in range(2 * count):
        load(slot).start()
    for slot in range(2 * count):
        load(slot).wait()
        into_out = first if slot < count else jnp.logical_not(first)
        for quad in range(4):
            pl.when(into_out)(lambda: store(slot, True, quad).start())
            pl.when(jnp.logical_not(into_out))(lambda: store(slot, False, quad).start())
    for slot in range(2 * count):
        for quad in range(4):
            store(slot, True, quad).wait()


def place_sums(core, owns, others):
    count = len(owns)
    quarter, width = owns[0].shape[1:]
    return pl.pallas_call(
        place_kernel,
        out_shape=(
            jax.ShapeDtypeStruct((count * width, width), jnp.float32),
            jax.ShapeDtypeStruct((width, count * width), jnp.float32),
        ),
        grid_spec=pltpu.PrefetchScalarGridSpec(
            num_scalar_prefetch=1,
            grid=(1,),
            in_specs=[ANY] * (2 * count),
            out_specs=(ANY, ANY),
            scratch_shapes=[
                pltpu.VMEM((2 * count, 4, quarter, width), jnp.float32),
                pltpu.SemaphoreType.DMA((2 * count,)),
                pltpu.SemaphoreType.DMA((2 * count, 4)),
            ],
        ),
        compiler_params=pltpu.CompilerParams(dimension_semantics=('arbitrary',), vmem_limit_bytes=VMEM_LIMIT),
        cost_estimate=pl.CostEstimate(flops=20 * width * width * count, bytes_accessed=16 * width * width * count, transcendentals=0),
        name='place_sums',
    )(core, *owns, *others)


def solution(mesh):
    def device_step(x_one, z_one, x_two, z_two, grad_out, w1_in, w1_out, w2_in, w2_out):
        width = grad_out.shape[1]
        count = w1_out.shape[0] // width
        core = lax.axis_index('group').astype(jnp.int32).reshape(1)
        owns, others = [], []
        waiting = None

        def carry():
            if waiting is None:
                return None
            return (*waiting, owns[-1] if owns else None)

        def collect(load, results):
            if load is not None:
                owns.append(results[0])
            if len(results) > 1:
                others.append(results[1])

        def block(x_in, z_pre, grad_y, w_in, w_out, base):
            nonlocal waiting
            dz_parts = []
            for part in range(count):
                load = carry()
                dz, keep, send, *results = chunk_grads(z_pre, grad_y, x_in, w_out, part, load, base + part)
                collect(load, results)
                waiting = (keep, send)
                dz_parts.append(dz)
            load = carry()
            dx, *results = input_grad(grad_y, dz_parts, w_in, load, base + count)
            collect(load, results)
            waiting = None
            return dx

        dx_two = block(x_two, z_two, grad_out, w2_in, w2_out, 0)
        dx_one = block(x_one, z_one, dx_two, w1_in, w1_out, count + 1)
        others.append(lax.ppermute(owns[-1], 'group', [(0, 1), (1, 0)]))
        sums_two = place_sums(core, owns[:count], others[:count])
        sums_one = place_sums(core, owns[count:], others[count:])
        return *sums_two, *sums_one, dx_one

    row_spec = P(AXES, None)
    repl_spec = P()
    return jax.shard_map(
        device_step,
        mesh=mesh,
        in_specs=(row_spec, row_spec, row_spec, row_spec, row_spec, repl_spec, repl_spec, repl_spec, repl_spec),
        out_specs=(repl_spec, repl_spec, repl_spec, repl_spec, row_spec),
        check_vma=False,
    )
```

time: 1190 us -> 556 us (0.47)
  waiting for transfers between devices: 621 us -> 0.01 us
  Pallas kernels: 0 us -> 534 us
  matrix products: 466 us -> 0 us
  blocking collectives: 35.6 us -> 0 us
  local copies, waits for them, and re-layouts: 28.2 us -> 11.9 us
  between operations: 14.8 us -> 1.18 us
  other arithmetic: 12.5 us -> 0 us
    pallas_call x0 -> x12, Pallas kernels: none -> 534 us  [the longest x8 399 us: chunk_grads(): pl.pallas_call(functools.partial(chunk_kernel, lane_mode(load)), out_shap...]
    dot_general x8 -> x0, matrix products: 466 us -> none  [the longest x2 157 us: block_backward(): lax.dot_general(grad_y, w_out, CONTRACT_COLS, preferred_element_type=jnp....]
    all_gather x12 -> x0, waiting for transfers between devices: 425 us -> none  [the longest x4 246 us: reduce_grad(): full_sum = lax.all_gather(full_sum, 'second', axis=0, tiled=True)]
    reduce_scatter x8 -> x0, waiting for transfers between devices: 194 us -> none  [the longest x4 136 us: reduce_grad(): lax.psum_scatter(part_sum, 'third', scatter_dimension=0, tiled=True)]
    all_to_all x4 -> x0, blocking collectives: 35.6 us -> none  [reduce_grad(): received = lax.all_to_all(pieces, 'group', 0, 0)]
    unnamed x12 -> x3, local copies, waits for them, and re-layouts: 28.2 us -> 11.9 us
    reduce_sum x4 -> x0, other arithmetic: 12.5 us -> none  [reduce_grad(): part_sum = jnp.sum(received, axis=0, dtype=jnp.float32)]
  transfers between devices with their start and end apart: 20 -> 1, of which waited for: 15 -> 0; matrix products, arithmetic and copies ran while one was open for 36% -> 0% of each run, Pallas kernels for 0% -> 2%
where the time goes in v2:
time: 556 us; the launch traced here: 548 us
  Pallas kernels  534 us (96%)
  local copies, waits for them, and re-layouts  11.9 us (2%)
    pallas_call x8, Pallas kernels, chunk_grads(): pl.pallas_call(functools.partial(chunk_kernel, lane_mode(load)), out_shap...  399 us
    pallas_call x2, Pallas kernels, input_grad(): pl.pallas_call(functools.partial(input_kernel, lane_mode(load), len(dz_pa...  108 us
    pallas_call x2, Pallas kernels, place_sums(): pl.pallas_call(place_kernel, out_shape=(jax.ShapeDtypeStruct((count * wid...  26.7 us
    unnamed x3, local copies, waits for them, and re-layouts  11.9 us
  transfers between devices with their start and end apart: 1, of which 0 were waited for; matrix products, arithmetic and copies ran while one was open for 0% of the time, Pallas kernels for 2%

profile of v2, /device:TPU:0, one launch (start us, length us, event | category | flops | bytes accessed | tf_op | source)
XLA Modules:
  0.0 547.5 jit_solution(17957062702521311677)
XLA Ops:
  0.6 42.4 %chunk_grads.8 = (bf16[8192,768]{1,0:T(8,128)(2,1)}, bf16[768,768]{1,0:T(8,128)(2,1)}, bf16[768,768]{1,0:T(8,128)(2,1)}) custom-call(bf16[8192,3072]{1,0:T(8,128)(2,1)} %refs_0_.12, bf16[8192,768]{1,0:T(8,128)(2,1)} %refs_0_.13, bf16[8192,768]{1,0:T(8,128)(2,1)} %refs_2_.11, bf16[3072,768]{1,0:T(8,128)(2,1)} %refs_3_.11), custom_call_target="tpu_custom_call" | custom-call | flops 28991029248 | bytes 50331648 | tf_op jit(solution)/shard_map/chunk_grads/pallas_call | solution.py:236
  43.1 54.8 %chunk_grads.9 = (bf16[8192,768]{1,0:T(8,128)(2,1)}, bf16[768,768]{1,0:T(8,128)(2,1)}, bf16[768,768]{1,0:T(8,128)(2,1)}, f32[4,192,768]{2,1,0:T(8,128)}) custom-call(bf16[8192,3072]{1,0:T(8,128)(2,1)} %refs_0_.12, bf16[8192,768]{1,0:T(8,128)(2,1)} %refs_0_.13, bf16[8192,768]{1,0:T(8,128)(2,1)} %refs_2_.11, bf16[3072,768]{1,0:T(8,128)(2,1)} %refs_3_.11, ...), custom_call_target="tpu_custom_call" | custom-call | flops 28991029248 | bytes 50331648 | tf_op jit(solution)/shard_map/chunk_grads/pallas_call | solution.py:236
  97.9 51.8 %chunk_grads.10 = (bf16[8192,768]{1,0:T(8,128)(2,1)}, bf16[768,768]{1,0:T(8,128)(2,1)}, bf16[768,768]{1,0:T(8,128)(2,1)}, f32[4,192,768]{2,1,0:T(8,128)}, f32[4,192,768]{2,1,0:T(8,128)}) custom-call(bf16[8192,3072]{1,0:T(8,128)(2,1)} %refs_0_.12, bf16[8192,768]{1,0:T(8,128)(2,1)} %refs_0_.13, bf16[8192,768]{1,0:T(8,128)(2,1)} %refs_2_.11, ...), custom_call_target="tpu_custom_call" | custom-call | flops 28991029248 | bytes 50331648 | tf_op jit(solution)/shard_map/chunk_grads/pallas_call | solution.py:236
  149.7 52.1 %chunk_grads.11 = (bf16[8192,768]{1,0:T(8,128)(2,1)}, bf16[768,768]{1,0:T(8,128)(2,1)}, bf16[768,768]{1,0:T(8,128)(2,1)}, f32[4,192,768]{2,1,0:T(8,128)}, f32[4,192,768]{2,1,0:T(8,128)}) custom-call(bf16[8192,3072]{1,0:T(8,128)(2,1)} %refs_0_.12, bf16[8192,768]{1,0:T(8,128)(2,1)} %refs_0_.13, bf16[8192,768]{1,0:T(8,128)(2,1)} %refs_2_.11, ...), custom_call_target="tpu_custom_call" | custom-call | flops 28991029248 | bytes 50331648 | tf_op jit(solution)/shard_map/chunk_grads/pallas_call | solution.py:236
  201.8 54.1 %input_grad.2 = (bf16[8192,768]{1,0:T(8,128)(2,1)}, f32[4,192,768]{2,1,0:T(8,128)}, f32[4,192,768]{2,1,0:T(8,128)}) custom-call(bf16[8192,768]{1,0:T(8,128)(2,1)} %refs_0_.13, bf16[8192,768]{1,0:T(8,128)(2,1)} %get-tuple-element.59.refs_1_, bf16[8192,768]{1,0:T(8,128)(2,1)} %get-tuple-element.60.refs_2_, bf16[8192,768]{1,0:T(8,128)(2,1)} %get-tuple-element.61.refs_3_, ...), custom_call_target="tpu_custom_call" | custom-call | flops 38654705664 | bytes 75497472 | tf_op jit(solution)/shard_map/input_grad/pallas_call | solution.py:289
  255.9 42.4 %chunk_grads.12 = (bf16[8192,768]{1,0:T(8,128)(2,1)}, bf16[768,768]{1,0:T(8,128)(2,1)}, bf16[768,768]{1,0:T(8,128)(2,1)}) custom-call(bf16[8192,3072]{1,0:T(8,128)(2,1)} %refs_0_.17, bf16[8192,768]{1,0:T(8,128)(2,1)} %get-tuple-element.69.refs_1_.refs_0_, bf16[8192,768]{1,0:T(8,128)(2,1)} %refs_2_.15, bf16[3072,768]{1,0:T(8,128)(2,1)} %refs_3_.15), custom_call_target="tpu_custom_call" | custom-call | flops 28991029248 | bytes 50331648 | tf_op jit(solution)/shard_map/chunk_grads/pallas_call | solution.py:236
  298.3 52.2 %chunk_grads.13 = (bf16[8192,768]{1,0:T(8,128)(2,1)}, bf16[768,768]{1,0:T(8,128)(2,1)}, bf16[768,768]{1,0:T(8,128)(2,1)}, f32[4,192,768]{2,1,0:T(8,128)}, f32[4,192,768]{2,1,0:T(8,128)}) custom-call(bf16[8192,3072]{1,0:T(8,128)(2,1)} %refs_0_.17, bf16[8192,768]{1,0:T(8,128)(2,1)} %get-tuple-element.69.refs_1_.refs_0_, bf16[8192,768]{1,0:T(8,128)(2,1)} %refs_2_.15, ...), custom_call_target="tpu_custom_call" | custom-call | flops 28991029248 | bytes 50331648 | tf_op jit(solution)/shard_map/chunk_grads/pallas_call | solution.py:236
  350.5 51.8 %chunk_grads.14 = (bf16[8192,768]{1,0:T(8,128)(2,1)}, bf16[768,768]{1,0:T(8,128)(2,1)}, bf16[768,768]{1,0:T(8,128)(2,1)}, f32[4,192,768]{2,1,0:T(8,128)}, f32[4,192,768]{2,1,0:T(8,128)}) custom-call(bf16[8192,3072]{1,0:T(8,128)(2,1)} %refs_0_.17, bf16[8192,768]{1,0:T(8,128)(2,1)} %get-tuple-element.69.refs_1_.refs_0_, bf16[8192,768]{1,0:T(8,128)(2,1)} %refs_2_.15, ...), custom_call_target="tpu_custom_call" | custom-call | flops 28991029248 | bytes 50331648 | tf_op jit(solution)/shard_map/chunk_grads/pallas_call | solution.py:236
  402.3 51.9 %chunk_grads.15 = (bf16[8192,768]{1,0:T(8,128)(2,1)}, bf16[768,768]{1,0:T(8,128)(2,1)}, bf16[768,768]{1,0:T(8,128)(2,1)}, f32[4,192,768]{2,1,0:T(8,128)}, f32[4,192,768]{2,1,0:T(8,128)}) custom-call(bf16[8192,3072]{1,0:T(8,128)(2,1)} %refs_0_.17, bf16[8192,768]{1,0:T(8,128)(2,1)} %get-tuple-element.69.refs_1_.refs_0_, bf16[8192,768]{1,0:T(8,128)(2,1)} %refs_2_.15, ...), custom_call_target="tpu_custom_call" | custom-call | flops 28991029248 | bytes 50331648 | tf_op jit(solution)/shard_map/chunk_grads/pallas_call | solution.py:236
  454.2 54.3 %input_grad.3 = (bf16[8192,768]{1,0:T(8,128)(2,1)}, f32[4,192,768]{2,1,0:T(8,128)}, f32[4,192,768]{2,1,0:T(8,128)}) custom-call(bf16[8192,768]{1,0:T(8,128)(2,1)} %get-tuple-element.69.refs_1_.refs_0_, bf16[8192,768]{1,0:T(8,128)(2,1)} %get-tuple-element.82.refs_1_, bf16[8192,768]{1,0:T(8,128)(2,1)} %get-tuple-element.83.refs_2_, ...), custom_call_target="tpu_custom_call" | custom-call | flops 38654705664 | bytes 75497472 | tf_op jit(solution)/shard_map/input_grad/pallas_call | solution.py:289
  508.5 0.0 collective-permute-start
  508.5 13.3 %place_sums.2 = (f32[3072,768]{1,0:T(8,128)}, f32[768,3072]{1,0:T(8,128)}) custom-call(s32[1]{0:T(128)} %bitcast.core_ref, f32[4,192,768]{2,1,0:T(8,128)} %get-tuple-element.52.refs_6_.refs_0_, f32[4,192,768]{2,1,0:T(8,128)} %get-tuple-element.55.refs_6_.refs_1_, f32[4,192,768]{2,1,0:T(8,128)} %get-tuple-element.58.refs_8_.refs_2_, ...), custom_call_target="tpu_custom_call" | custom-call | flops 47185920 | bytes 37748736 | tf_op jit(solution)/shard_map/place_sums/pallas_call | solution.py:337
  521.9 0.0 collective-permute-done.refs_7_
  521.9 0.0 copy-start
  521.9 1.4 copy-done
  523.3 13.3 %place_sums.3 = (f32[3072,768]{1,0:T(8,128)}, f32[768,3072]{1,0:T(8,128)}) custom-call(s32[1]{0:T(128)} %bitcast.core_ref, f32[4,192,768]{2,1,0:T(8,128)} %get-tuple-element.75.refs_6_.refs_0_, f32[4,192,768]{2,1,0:T(8,128)} %get-tuple-element.78.refs_6_.refs_1_, f32[4,192,768]{2,1,0:T(8,128)} %get-tuple-element.81.refs_8_.refs_2_, ...), custom_call_target="tpu_custom_call" | custom-call | flops 47185920 | bytes 37748736 | tf_op jit(solution)/shard_map/place_sums/pallas_call | solution.py:337
  536.6 10.5 %copy.15 = bf16[8192,768]{1,0:T(8,128)(2,1)} copy(bf16[8192,768]{1,0:T(8,128)(2,1)} %get-tuple-element.104) | data formatting | bytes 25165824
Async XLA Ops:
  508.5 13.4 %collective-permute-start = (f32[4,192,768]{2,1,0:T(8,128)}, f32[4,192,768]{2,1,0:T(8,128)S(1)}, u32[]{:S(2)}, u32[]{:S(2)}) collective-permute-start(f32[4,192,768]{2,1,0:T(8,128)} %get-tuple-element.88.refs_3_), channel_id=1, source_target_pairs={{0,1},{1,0},{2,3},{3,2},{4,5},{5,4},{6,7},{7,6}} | collective-permute-start | bytes 7077896 | tf_op jit(solution)/shard_map/ppermute | solution.py:396
  521.9 1.4 copy-start

commit v3 on v2

v3 whole, which is shorter than its diff:
```python
import functools
import math
import jax
import jax.numpy as jnp
from jax import lax
from jax.experimental import pallas as pl
from jax.experimental.pallas import tpu as pltpu
from jax.sharding import PartitionSpec as P

AXES = ('third', 'second', 'group')
INV_ROOT_TWO = math.sqrt(0.5)
INV_ROOT_TWO_PI = 1.0 / math.sqrt(2.0 * math.pi)
CONTRACT_ROWS = (((0,), (0,)), ((), ()))
CONTRACT_COLS = (((1,), (1,)), ((), ()))
TM = 512
VMEM_LIMIT = 60 * 1024 * 1024
MESH = pl.DeviceIdType.MESH
HALVES = 2
ROW_TILES = 8
ANY = pl.BlockSpec(memory_space=pl.ANY)


def dot(lhs, rhs, dims):
    return lax.dot_general(lhs, rhs, dims, preferred_element_type=jnp.float32)


def gelu_pair(z_pre):
    z_val = z_pre.astype(jnp.float32)
    cdf_val = 0.5 * (1.0 + lax.erf(z_val * INV_ROOT_TWO))
    hidden = (z_val * cdf_val).astype(jnp.bfloat16)
    slope = cdf_val + z_val * jnp.exp(-0.5 * z_val * z_val) * INV_ROOT_TWO_PI
    return hidden, slope


class Lane:
    def __init__(self, plan, ins, outs, scratch):
        ins, outs = list(ins), list(outs)
        self.new, self.old, self.done = plan
        if self.new:
            self.keep, self.send, self.own = ins.pop(0), ins.pop(0), outs.pop(0)
        if self.old:
            self.held, self.near_out = ins.pop(0), outs.pop(0)
        if self.done:
            self.final = (ins.pop(0), ins.pop(0))
            self.final_out = (outs.pop(0), outs.pop(0))
        self.recv_pair, self.cur, self.recv_one, self.mid, self.recv_two, self.fin, self.send_sem, self.recv_sem, self.copy_sem = scratch
        self.rows = self.cur.shape[1]
        self.half = self.rows // HALVES
        self.pos = (lax.axis_index('second'), lax.axis_index('third'))
        self.near = ({'second': 1 - self.pos[0]}, {'third': 1 - self.pos[1]})
        self.pair = {'group': 1 - lax.axis_index('group')}

    def remote(self, src, dst, slot, device):
        return pltpu.make_async_remote_copy(
            src_ref=src,
            dst_ref=dst,
            send_sem=self.send_sem.at[slot],
            recv_sem=self.recv_sem.at[slot],
            device_id=device,
            device_id_type=MESH,
        )

    def part(self, half):
        return pl.ds(half * self.half, self.half)

    def exchange(self):
        return self.remote(self.send, self.recv_pair, 0, self.pair)

    def scatter(self, side, half):
        src = self.cur.at[2 * side + 1 - self.pos[side], self.part(half)]
        return self.remote(src, self.recv_one.at[side, self.part(half)], 1 + 2 * side + half, self.near[side])

    def swap(self, side, half):
        src = self.mid.at[side, self.part(half)]
        return self.remote(src, self.recv_two.at[side, self.part(half)], 5 + 2 * side + half, self.near[1 - side])

    def gather(self, side):
        return self.remote(self.held.at[side], self.near_out.at[side], 9 + side, self.near[side])

    def join(self, index):
        return self.remote(self.final[index], self.final_out[index], 11 + index, self.pair)

    def result(self, half):
        return pltpu.make_async_copy(self.fin.at[:, self.part(half)], self.own.at[:, self.part(half)], self.copy_sem.at[half])

    def enter(self):
        barrier = pltpu.get_barrier_semaphore()
        for device in (self.pair, *self.near):
            pl.semaphore_signal(barrier, inc=1, device_id=device, device_id_type=MESH)
        pl.semaphore_wait(barrier, 3)
        if self.new:
            self.exchange().start()
        if self.old:
            for side in range(2):
                self.gather(side).start()
        if self.done:
            for index in range(2):
                self.join(index).start()

    def add_pair(self):
        self.exchange().wait_recv()

        def add(quarter, carry):
            rows = pl.ds(pl.multiple_of(quarter * self.rows, self.rows), self.rows)
            self.cur[quarter] = self.keep[rows, :].astype(jnp.float32) + self.recv_pair[rows, :].astype(jnp.float32)
            return carry

        lax.fori_loop(0, 4, add, 0)
        for half in range(HALVES):
            for side in range(2):
                self.scatter(side, half).start()

    def add_first(self, half):
        rows = self.part(half)
        for side in range(2):
            self.scatter(side, half).wait_recv()
            self.mid[side, rows, :] = self.cur[2 * side + self.pos[side], rows, :] + self.recv_one[side, rows, :]
            self.swap(side, half).start()

    def add_second(self, half):
        rows = self.part(half)
        for side in range(2):
            self.swap(side, half).wait_recv()
            self.fin[side, rows, :] = self.mid[side, rows, :] + self.recv_two[side, rows, :]
        self.result(half).start()

    def leave(self):
        if self.new:
            self.add_second(1)
        if self.old:
            for side in range(2):
                self.gather(side).wait()
        if self.done:
            for index in range(2):
                self.join(index).wait()
        if self.new:
            self.exchange().wait_send()
            for half in range(HALVES):
                for side in range(2):
                    self.scatter(side, half).wait_send()
                    self.swap(side, half).wait_send()
                self.result(half).wait()

    def before(self, step):
        pl.when(step == 0)(self.enter)
        if self.new:
            pl.when(step == 2)(self.add_pair)
            pl.when(step == 8)(lambda: self.add_first(0))
            pl.when(step == 11)(lambda: self.add_first(1))
            pl.when(step == 13)(lambda: self.add_second(0))

    def after(self, step):
        pl.when(step == pl.num_programs(0) - 1)(self.leave)


def lane_plan(load):
    return tuple(item is not None for item in load)


def lane_specs(load, width):
    new, old, done = load
    pieces = (2, width // 4, width)
    result = jax.ShapeDtypeStruct(pieces, jnp.float32)
    operands, in_specs, outs = [], [], []
    if new is not None:
        operands += new
        in_specs += [pl.BlockSpec((width, width), lambda i: (0, 0)), ANY]
        outs.append(result)
    if old is not None:
        operands.append(old)
        in_specs.append(ANY)
        outs.append(result)
    if done is not None:
        operands += done
        in_specs += [ANY, ANY]
        outs += [result, result]
    scratch = [
        pltpu.VMEM((width, width), jnp.bfloat16),
        pltpu.VMEM((4, *pieces[1:]), jnp.float32),
        pltpu.VMEM(pieces, jnp.float32),
        pltpu.VMEM(pieces, jnp.float32),
        pltpu.VMEM(pieces, jnp.float32),
        pltpu.VMEM(pieces, jnp.float32),
        pltpu.SemaphoreType.DMA((13,)),
        pltpu.SemaphoreType.DMA((13,)),
        pltpu.SemaphoreType.DMA((HALVES,)),
    ]
    return operands, in_specs, outs, [ANY] * len(outs), scratch if operands else []


def split_lane(plan, refs, n_in, n_out):
    new, old, done = plan
    refs = list(refs)
    extra_in, extra_out = 2 * new + old + 2 * done, new + old + 2 * done
    ins, refs = refs[:n_in], refs[n_in:]
    lane_in, refs = refs[:extra_in], refs[extra_in:]
    outs, refs = refs[:n_out], refs[n_out:]
    lane_out, refs = refs[:extra_out], refs[extra_out:]
    if not any(plan):
        return ins, outs, refs, None
    return ins, outs, refs[9:], Lane(plan, lane_in, lane_out, refs[:9])


def params(load, ident):
    extra = dict(collective_id=ident, has_side_effects=True) if any(lane_plan(load)) else {}
    return pltpu.CompilerParams(dimension_semantics=('arbitrary',), vmem_limit_bytes=VMEM_LIMIT, **extra)


def chunk_kernel(plan, *refs):
    ins, outs, scratch, lane = split_lane(plan, refs, 4, 3)
    z_ref, dy_ref, x_ref, w_ref = ins
    dz_ref, keep_ref, send_ref = outs
    acc_o, acc_i, turned = scratch
    step = pl.program_id(0)
    if lane is not None:
        lane.before(step)

    @pl.when(step == 0)
    def _():
        acc_o[...] = jnp.zeros_like(acc_o)
        acc_i[...] = jnp.zeros_like(acc_i)
        turned[...] = w_ref[...].T

    hidden, slope = gelu_pair(z_ref[...])
    dz = (jnp.dot(dy_ref[...], turned[...], preferred_element_type=jnp.float32) * slope).astype(jnp.bfloat16)
    dz_ref[...] = dz
    acc_o[...] += dot(hidden, dy_ref[...], CONTRACT_ROWS)
    acc_i[...] += dot(x_ref[...], dz, CONTRACT_ROWS)

    @pl.when(step == pl.num_programs(0) - 1)
    def _():
        first = lax.axis_index('group') == 0
        block = acc_o.shape[0] // 6

        def store(out_ref, acc):
            def body(index, carry):
                rows = pl.ds(pl.multiple_of(index * block, block), block)
                out_ref[rows, :] = acc[rows, :].astype(jnp.bfloat16)
                return carry

            lax.fori_loop(0, 6, body, 0)

        @pl.when(first)
        def _():
            store(keep_ref, acc_o)
            store(send_ref, acc_i)

        @pl.when(jnp.logical_not(first))
        def _():
            store(keep_ref, acc_i)
            store(send_ref, acc_o)

    if lane is not None:
        lane.after(step)


def chunk_grads(z_pre, grad_y, x_in, w_out, part, load, ident):
    tokens, width = grad_y.shape
    square = pl.BlockSpec((width, width), lambda i: (0, 0))
    rows = pl.BlockSpec((TM, width), lambda i: (i, 0))
    operands, in_specs, outs, out_specs, scratch = lane_specs(load, width)
    flops = 6 * tokens * width * width
    return pl.pallas_call(
        functools.partial(chunk_kernel, lane_plan(load)),
        out_shape=[
            jax.ShapeDtypeStruct((tokens, width), jnp.bfloat16),
            jax.ShapeDtypeStruct((width, width), jnp.bfloat16),
            jax.ShapeDtypeStruct((width, width), jnp.bfloat16),
            *outs,
        ],
        grid=(tokens // TM,),
        in_specs=[
            pl.BlockSpec((TM, width), lambda i: (i, part)),
            rows,
            rows,
            pl.BlockSpec((width, width), lambda i: (part, 0)),
            *in_specs,
        ],
        out_specs=[rows, square, square, *out_specs],
        scratch_shapes=[
            *scratch,
            pltpu.VMEM((width, width), jnp.float32),
            pltpu.VMEM((width, width), jnp.float32),
            pltpu.VMEM((width, width), jnp.bfloat16),
        ],
        compiler_params=params(load, ident),
        cost_estimate=pl.CostEstimate(flops=flops, bytes_accessed=8 * tokens * width, transcendentals=2 * tokens * width),
        name='chunk_grads',
    )(z_pre, grad_y, x_in, w_out, *operands)


def input_kernel(plan, count, *refs):
    ins, outs, scratch, lane = split_lane(plan, refs, 2 + count, 1)
    dy_ref, *dz_refs, w_ref = ins
    (turned,) = scratch
    step = pl.program_id(0)
    if lane is not None:
        lane.before(step)

    @pl.when(step == 0)
    def _():
        turned[...] = w_ref[...].T

    total = dy_ref[...].astype(jnp.float32)
    dz = jnp.concatenate([ref[...] for ref in dz_refs], axis=1)
    total = total + jnp.dot(dz, turned[...], preferred_element_type=jnp.float32)
    outs[0][...] = total.astype(jnp.bfloat16)
    if lane is not None:
        lane.after(step)


def input_grad(grad_y, dz_parts, w_in, load, ident):
    tokens, width = grad_y.shape
    rows = pl.BlockSpec((TM, width), lambda i: (i, 0))
    operands, in_specs, outs, out_specs, scratch = lane_specs(load, width)
    return pl.pallas_call(
        functools.partial(input_kernel, lane_plan(load), len(dz_parts)),
        out_shape=[jax.ShapeDtypeStruct((tokens, width), jnp.bfloat16), *outs],
        grid=(tokens // TM,),
        in_specs=[rows] * (1 + len(dz_parts)) + [pl.BlockSpec(w_in.shape, lambda i: (0, 0)), *in_specs],
        out_specs=[rows, *out_specs],
        scratch_shapes=[*scratch, pltpu.VMEM(w_in.shape[::-1], jnp.bfloat16)],
        compiler_params=params(load, ident),
        cost_estimate=pl.CostEstimate(flops=2 * tokens * width * w_in.shape[1], bytes_accessed=12 * tokens * width, transcendentals=0),
        name='input_grad',
    )(grad_y, *dz_parts, w_in, *operands)


def place_kernel(layout, width, has_rows, where_ref, *refs):
    refs = list(refs)
    pieces, refs = refs[:len(layout)], refs[len(layout):]
    rows_in = refs.pop(0) if has_rows else None
    sum_out, sum_in = refs[:2]
    refs = refs[2:]
    rows_out = refs.pop(0) if has_rows else None
    held, in_sem, out_sem, *rest = refs
    quarter = width // 4
    first = where_ref[0] == 0

    def load(index):
        place = held.at[index, pl.ds(0, pieces[index].shape[0])]
        return pltpu.make_async_copy(pieces[index], place, in_sem.at[index])

    def store(index, entry, into_out):
        part, sides, _, far = layout[index]
        side = sides[entry]
        pos = where_ref[1 + side]
        row = pl.multiple_of((2 * side + (1 - pos if far else pos)) * quarter, quarter)
        if into_out:
            dst = sum_out.at[pl.ds(part * width + row, quarter), :]
        else:
            dst = sum_in.at[pl.ds(row, quarter), pl.ds(part * width, width)]
        return pltpu.make_async_copy(held.at[index, entry], dst, out_sem.at[index, entry])

    def row_copy(tile, back):
        span = rows_in.shape[0] // ROW_TILES
        part = pl.ds(tile * span, span)
        rows_held, rows_sem = rest
        src, dst = (rows_held, rows_out) if back else (rows_in, rows_held)
        return pltpu.make_async_copy(src.at[part], dst.at[part], rows_sem.at[back, tile])

    for index in range(len(layout)):
        load(index).start()
    if has_rows:
        for tile in range(ROW_TILES):
            row_copy(tile, 0).start()
    for index, (_, sides, own, _) in enumerate(layout):
        load(index).wait()
        into_out = first if own else jnp.logical_not(first)
        for entry in range(len(sides)):
            pl.when(into_out)(lambda: store(index, entry, True).start())
            pl.when(jnp.logical_not(into_out))(lambda: store(index, entry, False).start())
    if has_rows:
        for tile in range(ROW_TILES):
            row_copy(tile, 0).wait()
            row_copy(tile, 1).start()
    for index, (_, sides, _, _) in enumerate(layout):
        for entry in range(len(sides)):
            store(index, entry, True).wait()
    if has_rows:
        for tile in range(ROW_TILES):
            row_copy(tile, 1).wait()


def place_sums(where, entries, count, rows=None):
    arrays = [entry[0] for entry in entries]
    layout = tuple(entry[1:] for entry in entries)
    quarter, width = arrays[0].shape[1:]
    out_shape = [
        jax.ShapeDtypeStruct((count * width, width), jnp.float32),
        jax.ShapeDtypeStruct((width, count * width), jnp.float32),
    ]
    scratch = [
        pltpu.VMEM((len(arrays), 2, quarter, width), jnp.float32),
        pltpu.SemaphoreType.DMA((len(arrays),)),
        pltpu.SemaphoreType.DMA((len(arrays), 2)),
    ]
    if rows is not None:
        arrays.append(rows)
        out_shape.append(jax.ShapeDtypeStruct(rows.shape, rows.dtype))
        scratch += [pltpu.VMEM(rows.shape, rows.dtype), pltpu.SemaphoreType.DMA((2, ROW_TILES))]
    return pl.pallas_call(
        functools.partial(place_kernel, layout, width, rows is not None),
        out_shape=out_shape,
        grid_spec=pltpu.PrefetchScalarGridSpec(
            num_scalar_prefetch=1,
            grid=(1,),
            in_specs=[ANY] * len(arrays),
            out_specs=[ANY] * len(out_shape),
            scratch_shapes=scratch,
        ),
        compiler_params=pltpu.CompilerParams(dimension_semantics=('arbitrary',), vmem_limit_bytes=VMEM_LIMIT),
        cost_estimate=pl.CostEstimate(flops=6 * 8192 * width * width, bytes_accessed=16 * width * width * count, transcendentals=0),
        name='place_sums',
    )(where, *arrays)


def flip(value, axis):
    return lax.ppermute(value, axis, [(0, 1), (1, 0)])


def solution(mesh):
    def device_step(x_one, z_one, x_two, z_two, grad_out, w1_in, w1_out, w2_in, w2_out):
        width = grad_out.shape[1]
        count = w1_out.shape[0] // width
        where = jnp.stack([lax.axis_index(name).astype(jnp.int32) for name in ('group', 'second', 'third')])
        mine, near, mates = {}, {}, {}
        fresh = {}

        def take():
            new = next((n for n in sorted(fresh) if n not in mine), None)
            old = next((n for n in sorted(mine) if n not in near), None)
            done = next((n for n in sorted(near) if n not in mates), None)
            load = (
                None if new is None else fresh[new],
                None if old is None else mine[old],
                None if done is None else (mine[done], near[done]),
            )

            def file(results):
                results = list(results)
                if new is not None:
                    mine[new] = results.pop(0)
                if old is not None:
                    near[old] = results.pop(0)
                if done is not None:
                    mates[done] = (results.pop(0), results.pop(0))

            return load, file

        def block(x_in, z_pre, grad_y, w_in, w_out, base, ident):
            dz_parts = []
            for part in range(count):
                load, file = take()
                dz, keep, send, *results = chunk_grads(z_pre, grad_y, x_in, w_out, part, load, ident + part)
                file(results)
                fresh[base + part] = [keep, send]
                dz_parts.append(dz)
            load, file = take()
            dx, *results = input_grad(grad_y, dz_parts, w_in, load, ident + count)
            file(results)
            return dx

        dx_two = block(x_two, z_two, grad_out, w2_in, w2_out, 0, 0)
        dx_one = block(x_one, z_one, dx_two, w1_in, w1_out, count, count + 1)

        both = (0, 1)
        last = 2 * count - 1
        sides = [flip(mine[last][side:side + 1], axis) for side, axis in enumerate(('second', 'third'))]
        for n in near:
            if n not in mates:
                mates[n] = (flip(mine[n], 'group'), flip(near[n], 'group'))
        mate_last = flip(mine[last], 'group')

        def entries(n):
            part = n % count
            return [
                (mine[n], part, both, True, False),
                (near[n], part, both, True, True),
                (mates[n][0], part, both, False, False),
                (mates[n][1], part, both, False, True),
            ]

        *sums_two, dx_one = place_sums(where, sum([entries(n) for n in range(count)], []), count, dx_one)
        *sides, dx_one = lax.optimization_barrier((*sides, dx_one))
        late = [(mine[last], count - 1, both, True, False), (mate_last, count - 1, both, False, False)]
        for side, piece in enumerate(sides):
            late += [(piece, count - 1, (side,), True, True), (flip(piece, 'group'), count - 1, (side,), False, True)]
        sums_one = place_sums(where, [*sum([entries(n) for n in range(count, last)], []), *late], count)
        return *sums_two, *sums_one, dx_one

    row_spec = P(AXES, None)
    repl_spec = P()
    return jax.shard_map(
        device_step,
        mesh=mesh,
        in_specs=(row_spec, row_spec, row_spec, row_spec, row_spec, repl_spec, repl_spec, repl_spec, repl_spec),
        out_specs=(repl_spec, repl_spec, repl_spec, repl_spec, row_spec),
        check_vma=False,
    )
```

time: 556 us -> 524 us (0.942); the launches traced: 548 us -> 524 us
  Pallas kernels: 534 us -> 514 us
  local copies, waits for them, and re-layouts: 11.9 us -> 2.61 us
    pallas_call x12, Pallas kernels: 534 us -> 514 us  [the longest x8 374 us: chunk_grads(): pl.pallas_call(functools.partial(chunk_kernel, lane_plan(load)), out_shap...]
    unnamed x3 -> x8, local copies, waits for them, and re-layouts: 11.9 us -> 1.2 us
  transfers between devices with their start and end apart: 1 -> 7, of which waited for: 0 -> 2; matrix products, arithmetic and copies ran while one was open for 0% -> 0% of each run, Pallas kernels for 2% -> 14%
where the time goes in v3:
time: 524 us
  Pallas kernels  514 us (98%)
    pallas_call x8, Pallas kernels, chunk_grads(): pl.pallas_call(functools.partial(chunk_kernel, lane_plan(load)), out_shap...  374 us
    pallas_call x2, Pallas kernels, input_grad(): pl.pallas_call(functools.partial(input_kernel, lane_plan(load), len(dz_pa...  105 us
    pallas_call x2, Pallas kernels, place_sums(): pl.pallas_call(functools.partial(place_kernel, layout, width, rows is not...  35.5 us
  transfers between devices with their start and end apart: 7, of which 2 were waited for; matrix products, arithmetic and copies ran while one was open for 0% of the time, Pallas kernels for 14%

profile of v3, /device:TPU:0, one launch (start us, length us, event | category | flops | bytes accessed | tf_op | source)
XLA Modules:
  0.0 523.7 jit_solution(13485034339990099461)
XLA Ops:
  0.6 42.5 %chunk_grads.8 = (bf16[8192,768]{1,0:T(8,128)(2,1)}, bf16[768,768]{1,0:T(8,128)(2,1)}, bf16[768,768]{1,0:T(8,128)(2,1)}) custom-call(bf16[8192,3072]{1,0:T(8,128)(2,1)} %refs_0_.12, bf16[8192,768]{1,0:T(8,128)(2,1)} %refs_0_.13, bf16[8192,768]{1,0:T(8,128)(2,1)} %refs_2_.11, bf16[3072,768]{1,0:T(8,128)(2,1)} %refs_3_.11), custom_call_target="tpu_custom_call" | custom-call | flops 28991029248 | bytes 50331648 | tf_op jit(solution)/shard_map/chunk_grads/pallas_call | solution.py:263
  43.1 48.5 %chunk_grads.9 = (bf16[8192,768]{1,0:T(8,128)(2,1)}, bf16[768,768]{1,0:T(8,128)(2,1)}, bf16[768,768]{1,0:T(8,128)(2,1)}, f32[2,192,768]{2,1,0:T(8,128)}) custom-call(bf16[8192,3072]{1,0:T(8,128)(2,1)} %refs_0_.12, bf16[8192,768]{1,0:T(8,128)(2,1)} %refs_0_.13, bf16[8192,768]{1,0:T(8,128)(2,1)} %refs_2_.11, bf16[3072,768]{1,0:T(8,128)(2,1)} %refs_3_.11, ...), custom_call_target="tpu_custom_call" | custom-call | flops 28991029248 | bytes 50331648 | tf_op jit(solution)/shard_map/chunk_grads/pallas_call | solution.py:263
  91.7 48.1 %chunk_grads.10 = (bf16[8192,768]{1,0:T(8,128)(2,1)}, bf16[768,768]{1,0:T(8,128)(2,1)}, bf16[768,768]{1,0:T(8,128)(2,1)}, f32[2,192,768]{2,1,0:T(8,128)}, f32[2,192,768]{2,1,0:T(8,128)}) custom-call(bf16[8192,3072]{1,0:T(8,128)(2,1)} %refs_0_.12, bf16[8192,768]{1,0:T(8,128)(2,1)} %refs_0_.13, bf16[8192,768]{1,0:T(8,128)(2,1)} %refs_2_.11, ...), custom_call_target="tpu_custom_call" | custom-call | flops 28991029248 | bytes 50331648 | tf_op jit(solution)/shard_map/chunk_grads/pallas_call | solution.py:263
  139.7 48.2 %chunk_grads.11 = (bf16[8192,768]{1,0:T(8,128)(2,1)}, bf16[768,768]{1,0:T(8,128)(2,1)}, bf16[768,768]{1,0:T(8,128)(2,1)}, f32[2,192,768]{2,1,0:T(8,128)}, f32[2,...) custom-call(bf16[8192,3072]{1,0:T(8,128)(2,1)} %refs_0_.12, bf16[8192,768]{1,0:T(8,128)(2,1)} %refs_0_.13, ...), custom_call_target="tpu_custom_call" | custom-call | flops 28991029248 | bytes 50331648 | tf_op jit(solution)/shard_map/chunk_grads/pallas_call | solution.py:263
  188.0 52.7 %input_grad.2 = (bf16[8192,768]{1,0:T(8,128)(2,1)}, f32[2,192,768]{2,1,0:T(8,128)}, f32[2,192,768]{2,1,0:T(8,128)}, f32[2,192,768]{2,1,0:T(8,128)}, f32[2,192,768]{2,1,0:T(8,128)}) custom-call(bf16[8192,768]{1,0:T(8,128)(2,1)} %refs_0_.13, bf16[8192,768]{1,0:T(8,128)(2,1)} %get-tuple-element.78.refs_1_, bf16[8192,768]{1,0:T(8,128)(2,1)} %get-tuple-element.79.refs_2_, ...), custom_call_target="tpu_custom_call" | custom-call | flops 38654705664 | bytes 75497472 | tf_op jit(solution)/shard_map/input_grad/pallas_call | solution.py:316
  240.7 43.9 %chunk_grads.12 = (bf16[8192,768]{1,0:T(8,128)(2,1)}, bf16[768,768]{1,0:T(8,128)(2,1)}, bf16[768,768]{1,0:T(8,128)(2,1)}, f32[2,192,768]{2,1,0:T(8,128)}, f32[2,...) custom-call(bf16[8192,3072]{1,0:T(8,128)(2,1)} %refs_0_.17, bf16[8192,768]{1,0:T(8,128)(2,1)} %get-tuple-element.88.refs_1_.refs_0_, ...), custom_call_target="tpu_custom_call" | custom-call | flops 28991029248 | bytes 50331648 | tf_op jit(solution)/shard_map/chunk_grads/pallas_call | solution.py:263
  284.6 46.8 %chunk_grads.13 = (bf16[8192,768]{1,0:T(8,128)(2,1)}, bf16[768,768]{1,0:T(8,128)(2,1)}, bf16[768,768]{1,0:T(8,128)(2,1)}, f32[2,192,768]{2,1,0:T(8,128)}, f32[2,...) custom-call(bf16[8192,3072]{1,0:T(8,128)(2,1)} %refs_0_.17, bf16[8192,768]{1,0:T(8,128)(2,1)} %get-tuple-element.88.refs_1_.refs_0_, ...), custom_call_target="tpu_custom_call" | custom-call | flops 28991029248 | bytes 50331648 | tf_op jit(solution)/shard_map/chunk_grads/pallas_call | solution.py:263
  331.4 48.1 %chunk_grads.14 = (bf16[8192,768]{1,0:T(8,128)(2,1)}, bf16[768,768]{1,0:T(8,128)(2,1)}, bf16[768,768]{1,0:T(8,128)(2,1)}, f32[2,192,768]{2,1,0:T(8,128)}, f32[2,192,768]{2,1,0:T(8,128)}) custom-call(bf16[8192,3072]{1,0:T(8,128)(2,1)} %refs_0_.17, bf16[8192,768]{1,0:T(8,128)(2,1)} %get-tuple-element.88.refs_1_.refs_0_, bf16[8192,768]{1,0:T(8,128)(2,1)} %refs_2_.15, ...), custom_call_target="tpu_custom_call" | custom-call | flops 28991029248 | bytes 50331648 | tf_op jit(solution)/shard_map/chunk_grads/pallas_call | solution.py:263
  379.5 48.1 %chunk_grads.15 = (bf16[8192,768]{1,0:T(8,128)(2,1)}, bf16[768,768]{1,0:T(8,128)(2,1)}, bf16[768,768]{1,0:T(8,128)(2,1)}, f32[2,192,768]{2,1,0:T(8,128)}, f32[2,...) custom-call(bf16[8192,3072]{1,0:T(8,128)(2,1)} %refs_0_.17, ...), custom_call_target="tpu_custom_call" | custom-call | flops 28991029248 | bytes 50331648 | tf_op jit(solution)/shard_map/chunk_grads/pallas_call | solution.py:263
  427.5 0.0 collective-permute-start
  427.6 52.0 %input_grad.3 = (bf16[8192,768]{1,0:T(8,128)(2,1)}, f32[2,192,768]{2,1,0:T(8,128)}, f32[2,192,768]{2,1,0:T(8,128)}, f32[2,192,768]{2,1,0:T(8,128)}, f32[2,192,768]{2,1,0:T(8,128)}) custom-call(bf16[8192,768]{1,0:T(8,128)(2,1)} %get-tuple-element.88.refs_1_.refs_0_, bf16[8192,768]{1,0:T(8,128)(2,1)} %get-tuple-element.97.refs_1_, ...), custom_call_target="tpu_custom_call" | custom-call | flops 38654705664 | bytes 75497472 | tf_op jit(solution)/shard_map/input_grad/pallas_call | solution.py:316
  479.6 0.0 copy-start.1
  479.6 0.0 collective-permute-start.2
  479.6 1.4 fusion
  481.1 1.5 collective-permute-start.3
  482.6 0.5 collective-permute-start.4
  483.1 0.0 copy-done.1
  483.1 0.0 collective-permute-start.1
  483.1 0.6 pad_add_fusion.where_ref
  483.7 21.6 %place_sums.2 = (f32[3072,768]{1,0:T(8,128)}, f32[768,3072]{1,0:T(8,128)}, bf16[8192,768]{1,0:T(8,128)(2,1)}) custom-call(s32[3]{0:T(128)} %pad_add_fusion.where_ref, f32[2,192,768]{2,1,0:T(8,128)} %get-tuple-element.68.refs_6_.refs_7_.refs_0_, f32[2,192,768]{2,1,0:T(8,128)} %get-tuple-element.71.refs_8_.refs_1_, f32[2,192,768]{2,1,0:T(8,128)} %get-tuple-element.75.refs_2_, ...), custom_call_target="tpu_custom_call" | custom-call | flops 28991029248 | bytes 37748736 | tf_op jit(solution)/shard_map/place_sums/pallas_call | solution.py:402
  505.3 0.0 collective-permute-done.3.refs_14_
  505.3 0.0 collective-permute-done.4.refs_16_
  505.3 0.5 collective-permute-start.5
  505.9 0.0 collective-permute-start.6
  505.9 1.6 collective-permute-done.5.refs_15_
  507.5 0.0 copy-start.2
  507.5 0.8 collective-permute-done.6.refs_17_
  508.3 0.0 copy-start.3
  508.3 0.0 collective-permute-done.1.refs_11_
  508.4 0.0 collective-permute-done.2.refs_13_
  508.4 0.0 collective-permute-done.refs_10_
  508.4 0.0 copy-start
  508.4 0.0 copy-done.2
  508.4 0.8 copy-done.3
  509.2 0.4 copy-done
  509.6 13.9 %place_sums.3 = (f32[3072,768]{1,0:T(8,128)}, f32[768,3072]{1,0:T(8,128)}) custom-call(s32[3]{0:T(128)} %pad_add_fusion.where_ref, f32[2,192,768]{2,1,0:T(8,128)} %get-tuple-element.101.refs_6_.refs_7_.refs_0_, f32[2,192,768]{2,1,0:T(8,128)} %get-tuple-element.106.refs_8_.refs_1_, f32[2,192,768]{2,1,0:T(8,128)} %get-tuple-element.115.refs_2_, ...), custom_call_target="tpu_custom_call" | custom-call | flops 28991029248 | bytes 37748736 | tf_op jit(solution)/shard_map/place_sums/pallas_call | solution.py:402
Async XLA Ops:
  427.5 80.8 %collective-permute-start = (f32[2,192,768]{2,1,0:T(8,128)}, f32[2,192,768]{2,1,0:T(8,128)S(1)}, u32[]{:S(2)}, u32[]{:S(2)}) collective-permute-start(f32[2,192,768]{2,1,0:T(8,128)} %get-tuple-element.110.refs_8_), channel_id=1, source_target_pairs={{0,1},{1,0},{2,3},{3,2},{4,5},{5,4},{6,7},{7,6}} | collective-permute-start | bytes 3538952 | tf_op jit(solution)/shard_map/ppermute | solution.py:419
  479.6 3.5 copy-start.1
  479.6 28.7 %collective-permute-start.2 = (f32[2,192,768]{2,1,0:T(8,128)}, f32[2,192,768]{2,1,0:T(8,128)}, u32[]{:S(2)}, u32[]{:S(2)}) collective-permute-start(f32[2,192,768]{2,1,0:T(8,128)} %get-tuple-element.120.refs_12_), channel_id=1, source_target_pairs={{0,1},{1,0},{2,3},{3,2},{4,5},{5,4},{6,7},{7,6}} | collective-permute-start | bytes 3538952 | tf_op jit(solution)/shard_map/ppermute | solution.py:419
  481.1 24.3 %collective-permute-start.3 = (f32[1,192,768]{2,1,0:T(8,128)S(1)}, f32[1,192,768]{2,1,0:T(8,128)}, u32[]{:S(2)}, u32[]{:S(2)}) collective-permute-start(f32[1,192,768]{2,1,0:T(8,128)S(1)} %get-tuple-element.128), channel_id=1, source_target_pairs={{0,2},{2,0},{1,3},{3,1},{4,6},{6,4},{5,7},{7,5}} | collective-permute-start | bytes 1769480 | tf_op jit(solution)/shard_map/ppermute | solution.py:419
  482.6 22.8 %collective-permute-start.4 = (f32[1,192,768]{2,1,0:T(8,128)S(1)}, f32[1,192,768]{2,1,0:T(8,128)}, u32[]{:S(2)}, u32[]{:S(2)}) collective-permute-start(f32[1,192,768]{2,1,0:T(8,128)S(1)} %get-tuple-element.127), channel_id=1, source_target_pairs={{0,4},{4,0},{1,5},{5,1},{2,6},{6,2},{3,7},{7,3}} | collective-permute-start | bytes 1769480 | tf_op jit(solution)/shard_map/ppermute | solution.py:419
  483.1 25.2 %collective-permute-start.1 = (f32[2,192,768]{2,1,0:T(8,128)S(1)}, f32[2,192,768]{2,1,0:T(8,128)}, u32[]{:S(2)}, u32[]{:S(2)}) collective-permute-start(f32[2,192,768]{2,1,0:T(8,128)S(1)} %copy-done.1), channel_id=1, source_target_pairs={{0,1},{1,0},{2,3},{3,2},{4,5},{5,4},{6,7},{7,6}} | collective-permute-start | bytes 3538952 | tf_op jit(solution)/shard_map/ppermute | solution.py:419
  505.3 2.2 collective-permute-start.5
  505.9 2.5 collective-permute-start.6
  507.5 0.9 copy-start.2
  508.3 0.9 copy-start.3
  508.4 1.2 copy-start

commit v4 on v3

--- a/solution.py
+++ b/solution.py
@@ -9,10 +9,12 @@
 
 AXES = ('third', 'second', 'group')
 INV_ROOT_TWO = math.sqrt(0.5)
+HALF_LOG = -0.5 * math.log2(math.e)
 INV_ROOT_TWO_PI = 1.0 / math.sqrt(2.0 * math.pi)
 CONTRACT_ROWS = (((0,), (0,)), ((), ()))
 CONTRACT_COLS = (((1,), (1,)), ((), ()))
 TM = 512
+SUB = 256
 VMEM_LIMIT = 60 * 1024 * 1024
 MESH = pl.DeviceIdType.MESH
 HALVES = 2
@@ -26,9 +28,9 @@
 
 def gelu_pair(z_pre):
     z_val = z_pre.astype(jnp.float32)
-    cdf_val = 0.5 * (1.0 + lax.erf(z_val * INV_ROOT_TWO))
+    cdf_val = 0.5 * lax.erf(z_val * INV_ROOT_TWO) + 0.5
     hidden = (z_val * cdf_val).astype(jnp.bfloat16)
-    slope = cdf_val + z_val * jnp.exp(-0.5 * z_val * z_val) * INV_ROOT_TWO_PI
+    slope = cdf_val + (z_val * INV_ROOT_TWO_PI) * jnp.exp2(z_val * z_val * HALF_LOG)
     return hidden, slope
 
 
@@ -145,9 +147,9 @@
         pl.when(step == 0)(self.enter)
         if self.new:
             pl.when(step == 2)(self.add_pair)
-            pl.when(step == 8)(lambda: self.add_first(0))
+            pl.when(step == 9)(lambda: self.add_first(0))
             pl.when(step == 11)(lambda: self.add_first(1))
-            pl.when(step == 13)(lambda: self.add_second(0))
+            pl.when(step == 14)(lambda: self.add_second(0))
 
     def after(self, step):
         pl.when(step == pl.num_programs(0) - 1)(self.leave)
@@ -206,14 +208,75 @@
     return pltpu.CompilerParams(dimension_semantics=('arbitrary',), vmem_limit_bytes=VMEM_LIMIT, **extra)
 
 
-def chunk_kernel(plan, *refs):
-    ins, outs, scratch, lane = split_lane(plan, refs, 4, 3)
-    z_ref, dy_ref, x_ref, w_ref = ins
-    dz_ref, keep_ref, send_ref = outs
-    acc_o, acc_i, turned = scratch
+class Placer:
+    def __init__(self, layout, where, pieces, sum_out, sum_in, held, in_sem, out_sem):
+        self.layout, self.pieces, self.sum_out, self.sum_in = layout, pieces, sum_out, sum_in
+        self.held, self.in_sem, self.out_sem = held, in_sem, out_sem
+        core, *self.pos = where
+        self.first = core == 0
+
+    def load(self, index):
+        place = self.held.at[index, pl.ds(0, self.pieces[index].shape[0])]
+        return pltpu.make_async_copy(self.pieces[index], place, self.in_sem.at[index])
+
+    def store(self, index, entry, into_out):
+        part, sides, _, far = self.layout[index]
+        side = sides[entry]
+        width = self.sum_in.shape[0]
+        quarter = width // 4
+        pos = self.pos[side]
+        row = pl.multiple_of((2 * side + (1 - pos if far else pos)) * quarter, quarter)
+        if into_out:
+            dst = self.sum_out.at[pl.ds(part * width + row, quarter), :]
+        else:
+            dst = self.sum_in.at[pl.ds(row, quarter), pl.ds(part * width, width)]
+        return pltpu.make_async_copy(self.held.at[index, entry], dst, self.out_sem.at[index, entry])
+
+    def fetch(self):
+        for index in range(len(self.layout)):
+            self.load(index).start()
+
+    def place(self):
+        for index, (_, sides, own, _) in enumerate(self.layout):
+            self.load(index).wait()
+            into_out = self.first if own else jnp.logical_not(self.first)
+            for entry in range(len(sides)):
+                pl.when(into_out)(lambda: self.store(index, entry, True).start())
+                pl.when(jnp.logical_not(into_out))(lambda: self.store(index, entry, False).start())
+
+    def finish(self):
+        for index, (_, sides, _, _) in enumerate(self.layout):
+            for entry in range(len(sides)):
+                self.store(index, entry, True).wait()
+
+
+def place_scratch(arrays):
+    return [
+        pltpu.VMEM((len(arrays), 2, *arrays[0].shape[1:]), jnp.float32),
+        pltpu.SemaphoreType.DMA((len(arrays),)),
+        pltpu.SemaphoreType.DMA((len(arrays), 2)),
+    ]
+
+
+def place_shapes(count, width):
+    return [jax.ShapeDtypeStruct((count * width, width), jnp.float32), jax.ShapeDtypeStruct((width, count * width), jnp.float32)]
+
+
+def chunk_kernel(plan, layout, *refs):
+    hosted = len(layout)
+    ins, outs, scratch, lane = split_lane(plan, refs, 4 + hosted, 5 if hosted else 3)
+    z_ref, dy_ref, x_ref, w_ref, *pieces = ins
+    dz_ref, keep_ref, send_ref, *sums = outs
+    acc_o, acc_i, turned, *room = scratch
     step = pl.program_id(0)
     if lane is not None:
         lane.before(step)
+    if hosted:
+        where = [lax.axis_index(name) for name in ('group', 'second', 'third')]
+        placer = Placer(layout, where, pieces, *sums, *room)
+        pl.when(step == 2)(placer.fetch)
+        pl.when(step == 6)(placer.place)
+        pl.when(step == pl.num_programs(0) - 1)(placer.finish)
 
     @pl.when(step == 0)
     def _():
@@ -221,11 +284,16 @@
         acc_i[...] = jnp.zeros_like(acc_i)
         turned[...] = w_ref[...].T
 
-    hidden, slope = gelu_pair(z_ref[...])
-    dz = (jnp.dot(dy_ref[...], turned[...], preferred_element_type=jnp.float32) * slope).astype(jnp.bfloat16)
-    dz_ref[...] = dz
-    acc_o[...] += dot(hidden, dy_ref[...], CONTRACT_ROWS)
-    acc_i[...] += dot(x_ref[...], dz, CONTRACT_ROWS)
+    hidden_parts, dz_parts = [], []
+    for low in range(0, z_ref.shape[0], SUB):
+        part = pl.ds(low, SUB)
+        hidden, slope = gelu_pair(z_ref[part, :])
+        dz = (jnp.dot(dy_ref[part, :], turned[...], preferred_element_type=jnp.float32) * slope).astype(jnp.bfloat16)
+        dz_ref[part, :] = dz
+        hidden_parts.append(hidden)
+        dz_parts.append(dz)
+    acc_o[...] += dot(jnp.concatenate(hidden_parts, axis=0), dy_ref[...], CONTRACT_ROWS)
+    acc_i[...] += dot(x_ref[...], jnp.concatenate(dz_parts, axis=0), CONTRACT_ROWS)
 
     @pl.when(step == pl.num_programs(0) - 1)
     def _():
@@ -254,18 +322,22 @@
         lane.after(step)
 
 
-def chunk_grads(z_pre, grad_y, x_in, w_out, part, load, ident):
+def chunk_grads(z_pre, grad_y, x_in, w_out, part, load, ident, entries=()):
     tokens, width = grad_y.shape
     square = pl.BlockSpec((width, width), lambda i: (0, 0))
     rows = pl.BlockSpec((TM, width), lambda i: (i, 0))
     operands, in_specs, outs, out_specs, scratch = lane_specs(load, width)
+    pieces = [entry[0] for entry in entries]
+    layout = tuple(entry[1:] for entry in entries)
+    sums = place_shapes(w_out.shape[0] // width, width) if entries else []
     flops = 6 * tokens * width * width
     return pl.pallas_call(
-        functools.partial(chunk_kernel, lane_plan(load)),
+        functools.partial(chunk_kernel, lane_plan(load), layout),
         out_shape=[
             jax.ShapeDtypeStruct((tokens, width), jnp.bfloat16),
             jax.ShapeDtypeStruct((width, width), jnp.bfloat16),
             jax.ShapeDtypeStruct((width, width), jnp.bfloat16),
+            *sums,
             *outs,
         ],
         grid=(tokens // TM,),
@@ -274,19 +346,21 @@
             rows,
             rows,
             pl.BlockSpec((width, width), lambda i: (part, 0)),
+            *[ANY] * len(pieces),
             *in_specs,
         ],
-        out_specs=[rows, square, square, *out_specs],
+        out_specs=[rows, square, square, *[ANY] * len(sums), *out_specs],
         scratch_shapes=[
             *scratch,
             pltpu.VMEM((width, width), jnp.float32),
             pltpu.VMEM((width, width), jnp.float32),
             pltpu.VMEM((width, width), jnp.bfloat16),
+            *(place_scratch(pieces) if entries else []),
         ],
         compiler_params=params(load, ident),
         cost_estimate=pl.CostEstimate(flops=flops, bytes_accessed=8 * tokens * width, transcendentals=2 * tokens * width),
         name='chunk_grads',
-    )(z_pre, grad_y, x_in, w_out, *operands)
+    )(z_pre, grad_y, x_in, w_out, *pieces, *operands)
 
 
 def input_kernel(plan, count, *refs):
@@ -326,31 +400,16 @@
     )(grad_y, *dz_parts, w_in, *operands)
 
 
-def place_kernel(layout, width, has_rows, where_ref, *refs):
+def place_kernel(layout, has_base, has_rows, where_ref, *refs):
     refs = list(refs)
-    pieces, refs = refs[:len(layout)], refs[len(layout):]
+    pieces, refs = refs[:len(layout)], refs[len(layout) + 2 * has_base:]
     rows_in = refs.pop(0) if has_rows else None
     sum_out, sum_in = refs[:2]
     refs = refs[2:]
     rows_out = refs.pop(0) if has_rows else None
     held, in_sem, out_sem, *rest = refs
-    quarter = width // 4
-    first = where_ref[0] == 0
-
-    def load(index):
-        place = held.at[index, pl.ds(0, pieces[index].shape[0])]
-        return pltpu.make_async_copy(pieces[index], place, in_sem.at[index])
-
-    def store(index, entry, into_out):
-        part, sides, _, far = layout[index]
-        side = sides[entry]
-        pos = where_ref[1 + side]
-        row = pl.multiple_of((2 * side + (1 - pos if far else pos)) * quarter, quarter)
-        if into_out:
-            dst = sum_out.at[pl.ds(part * width + row, quarter), :]
-        else:
-            dst = sum_in.at[pl.ds(row, quarter), pl.ds(part * width, width)]
-        return pltpu.make_async_copy(held.at[index, entry], dst, out_sem.at[index, entry])
+    where = [where_ref[index] for index in range(3)]
+    placer = Placer(layout, where, pieces, sum_out, sum_in, held, in_sem, out_sem)
 
     def row_copy(tile, back):
         span = rows_in.shape[0] // ROW_TILES
@@ -359,48 +418,35 @@
         src, dst = (rows_held, rows_out) if back else (rows_in, rows_held)
         return pltpu.make_async_copy(src.at[part], dst.at[part], rows_sem.at[back, tile])
 
-    for index in range(len(layout)):
-        load(index).start()
+    placer.fetch()
     if has_rows:
         for tile in range(ROW_TILES):
             row_copy(tile, 0).start()
-    for index, (_, sides, own, _) in enumerate(layout):
-        load(index).wait()
-        into_out = first if own else jnp.logical_not(first)
-        for entry in range(len(sides)):
-            pl.when(into_out)(lambda: store(index, entry, True).start())
-            pl.when(jnp.logical_not(into_out))(lambda: store(index, entry, False).start())
+    placer.place()
     if has_rows:
         for tile in range(ROW_TILES):
             row_copy(tile, 0).wait()
             row_copy(tile, 1).start()
-    for index, (_, sides, _, _) in enumerate(layout):
-        for entry in range(len(sides)):
-            store(index, entry, True).wait()
+    placer.finish()
     if has_rows:
         for tile in range(ROW_TILES):
             row_copy(tile, 1).wait()
 
 
-def place_sums(where, entries, count, rows=None):
+def place_sums(where, entries, count, base=(), rows=None):
     arrays = [entry[0] for entry in entries]
     layout = tuple(entry[1:] for entry in entries)
-    quarter, width = arrays[0].shape[1:]
-    out_shape = [
-        jax.ShapeDtypeStruct((count * width, width), jnp.float32),
-        jax.ShapeDtypeStruct((width, count * width), jnp.float32),
-    ]
-    scratch = [
-        pltpu.VMEM((len(arrays), 2, quarter, width), jnp.float32),
-        pltpu.SemaphoreType.DMA((len(arrays),)),
-        pltpu.SemaphoreType.DMA((len(arrays), 2)),
-    ]
+    width = arrays[0].shape[2]
+    scratch = place_scratch(arrays)
+    out_shape = place_shapes(count, width)
+    aliases = {1 + len(arrays) + index: index for index in range(len(base))}
+    arrays += base
     if rows is not None:
         arrays.append(rows)
         out_shape.append(jax.ShapeDtypeStruct(rows.shape, rows.dtype))
         scratch += [pltpu.VMEM(rows.shape, rows.dtype), pltpu.SemaphoreType.DMA((2, ROW_TILES))]
     return pl.pallas_call(
-        functools.partial(place_kernel, layout, width, rows is not None),
+        functools.partial(place_kernel, layout, len(base) > 0, rows is not None),
         out_shape=out_shape,
         grid_spec=pltpu.PrefetchScalarGridSpec(
             num_scalar_prefetch=1,
@@ -409,6 +455,7 @@
             out_specs=[ANY] * len(out_shape),
             scratch_shapes=scratch,
         ),
+        input_output_aliases=aliases,
         compiler_params=pltpu.CompilerParams(dimension_semantics=('arbitrary',), vmem_limit_bytes=VMEM_LIMIT),
         cost_estimate=pl.CostEstimate(flops=6 * 8192 * width * width, bytes_accessed=16 * width * width * count, transcendentals=0),
         name='place_sums',
@@ -448,23 +495,35 @@
 
             return load, file
 
-        def block(x_in, z_pre, grad_y, w_in, w_out, base, ident):
-            dz_parts = []
+        both = (0, 1)
+
+        def own_entries(n):
+            return [(mine[n], n % count, both, True, False), (near[n], n % count, both, True, True)]
+
+        def mate_entries(n):
+            return [(mates[n][0], n % count, both, False, False), (mates[n][1], n % count, both, False, True)]
+
+        def block(x_in, z_pre, grad_y, w_in, w_out, base, ident, entries=()):
+            dz_parts, placed = [], []
             for part in range(count):
-                load, file = take()
-                dz, keep, send, *results = chunk_grads(z_pre, grad_y, x_in, w_out, part, load, ident + part)
-                file(results)
+                if part == 0:
+                    dz, keep, send, *placed = chunk_grads(z_pre, grad_y, x_in, w_out, part, (None, None, None), ident, entries)
+                else:
+                    load, file = take()
+                    dz, keep, send, *results = chunk_grads(z_pre, grad_y, x_in, w_out, part, load, ident + part)
+                    file(results)
                 fresh[base + part] = [keep, send]
                 dz_parts.append(dz)
             load, file = take()
             dx, *results = input_grad(grad_y, dz_parts, w_in, load, ident + count)
             file(results)
-            return dx
-
-        dx_two = block(x_two, z_two, grad_out, w2_in, w2_out, 0, 0)
-        dx_one = block(x_one, z_one, dx_two, w1_in, w1_out, count, count + 1)
-
-        both = (0, 1)
+            return dx, placed
+
+        dx_two, _ = block(x_two, z_two, grad_out, w2_in, w2_out, 0, 0)
+        early = [entry for n in sorted(near) for entry in own_entries(n)] + [entry for n in sorted(mates) for entry in mate_entries(n)]
+        own_done, mate_done = sorted(near), sorted(mates)
+        dx_one, placed = block(x_one, z_one, dx_two, w1_in, w1_out, count, count + 1, early)
+
         last = 2 * count - 1
         sides = [flip(mine[last][side:side + 1], axis) for side, axis in enumerate(('second', 'third'))]
         for n in near:
@@ -472,21 +531,16 @@
                 mates[n] = (flip(mine[n], 'group'), flip(near[n], 'group'))
         mate_last = flip(mine[last], 'group')
 
-        def entries(n):
-            part = n % count
-            return [
-                (mine[n], part, both, True, False),
-                (near[n], part, both, True, True),
-                (mates[n][0], part, both, False, False),
-                (mates[n][1], part, both, False, True),
-            ]
-
-        *sums_two, dx_one = place_sums(where, sum([entries(n) for n in range(count)], []), count, dx_one)
+        rest = []
+        for n in range(count):
+            rest += ([] if n in own_done else own_entries(n)) + ([] if n in mate_done else mate_entries(n))
+        *sums_two, dx_one = place_sums(where, rest, count, placed, dx_one)
         *sides, dx_one = lax.optimization_barrier((*sides, dx_one))
         late = [(mine[last], count - 1, both, True, False), (mate_last, count - 1, both, False, False)]
         for side, piece in enumerate(sides):
             late += [(piece, count - 1, (side,), True, True), (flip(piece, 'group'), count - 1, (side,), False, True)]
-        sums_one = place_sums(where, [*sum([entries(n) for n in range(count, last)], []), *late], count)
+        ready = [entry for n in range(count, last) for entry in own_entries(n) + mate_entries(n)]
+        sums_one = place_sums(where, ready + late, count)
         return *sums_two, *sums_one, dx_one
 
     row_spec = P(AXES, None)

time: 524 us -> 511 us (0.975)
  Pallas kernels: 514 us -> 501 us
    pallas_call x10, Pallas kernels: 410 us -> 396 us  [the longest x8 369 us: chunk_grads(): pl.pallas_call(functools.partial(chunk_kernel, lane_plan(load), layout),...]
  transfers between devices with their start and end apart: 7 -> 7, of which waited for: 2 -> 3; matrix products, arithmetic and copies ran while one was open for 0% -> 0% of each run, Pallas kernels for 14% -> 13%
where the time goes in v4:
time: 511 us
  Pallas kernels  501 us (98%)
    pallas_call x8, Pallas kernels, chunk_grads(): pl.pallas_call(functools.partial(chunk_kernel, lane_plan(load), layout),...  369 us
    pallas_call x2, Pallas kernels, input_grad(): pl.pallas_call(functools.partial(input_kernel, lane_plan(load), len(dz_pa...  105 us
    pallas_call x2, Pallas kernels, place_sums(): pl.pallas_call(functools.partial(place_kernel, layout, len(base) > 0, row...  27.7 us
  transfers between devices with their start and end apart: 7, of which 3 were waited for; matrix products, arithmetic and copies ran while one was open for 0% of the time, Pallas kernels for 13%

profile of v4, /device:TPU:0, one launch (start us, length us, event | category | flops | bytes accessed | tf_op | source)
XLA Modules:
  0.0 510.6 jit_solution(13361993475400851264)
XLA Ops:
  0.6 41.8 %chunk_grads.8 = (bf16[8192,768]{1,0:T(8,128)(2,1)}, bf16[768,768]{1,0:T(8,128)(2,1)}, bf16[768,768]{1,0:T(8,128)(2,1)}) custom-call(bf16[8192,3072]{1,0:T(8,128)(2,1)} %refs_0_.12, bf16[8192,768]{1,0:T(8,128)(2,1)} %refs_0_.13, bf16[8192,768]{1,0:T(8,128)(2,1)} %refs_2_.11, bf16[3072,768]{1,0:T(8,128)(2,1)} %refs_3_.11), custom_call_target="tpu_custom_call" | custom-call | flops 28991029248 | bytes 50331648 | tf_op jit(solution)/shard_map/chunk_grads/pallas_call | solution.py:334
  42.5 47.9 %chunk_grads.9 = (bf16[8192,768]{1,0:T(8,128)(2,1)}, bf16[768,768]{1,0:T(8,128)(2,1)}, bf16[768,768]{1,0:T(8,128)(2,1)}, f32[2,192,768]{2,1,0:T(8,128)}) custom-call(bf16[8192,3072]{1,0:T(8,128)(2,1)} %refs_0_.12, bf16[8192,768]{1,0:T(8,128)(2,1)} %refs_0_.13, bf16[8192,768]{1,0:T(8,128)(2,1)} %refs_2_.11, bf16[3072,768]{1,0:T(8,128)(2,1)} %refs_3_.11, ...), custom_call_target="tpu_custom_call" | custom-call | flops 28991029248 | bytes 50331648 | tf_op jit(solution)/shard_map/chunk_grads/pallas_call | solution.py:334
  90.3 46.5 %chunk_grads.10 = (bf16[8192,768]{1,0:T(8,128)(2,1)}, bf16[768,768]{1,0:T(8,128)(2,1)}, bf16[768,768]{1,0:T(8,128)(2,1)}, f32[2,192,768]{2,1,0:T(8,128)}, f32[2,192,768]{2,1,0:T(8,128)}) custom-call(bf16[8192,3072]{1,0:T(8,128)(2,1)} %refs_0_.12, bf16[8192,768]{1,0:T(8,128)(2,1)} %refs_0_.13, bf16[8192,768]{1,0:T(8,128)(2,1)} %refs_2_.11, ...), custom_call_target="tpu_custom_call" | custom-call | flops 28991029248 | bytes 50331648 | tf_op jit(solution)/shard_map/chunk_grads/pallas_call | solution.py:334
  136.8 46.5 %chunk_grads.11 = (bf16[8192,768]{1,0:T(8,128)(2,1)}, bf16[768,768]{1,0:T(8,128)(2,1)}, bf16[768,768]{1,0:T(8,128)(2,1)}, f32[2,192,768]{2,1,0:T(8,128)}, f32[2,...) custom-call(bf16[8192,3072]{1,0:T(8,128)(2,1)} %refs_0_.12, bf16[8192,768]{1,0:T(8,128)(2,1)} %refs_0_.13, ...), custom_call_target="tpu_custom_call" | custom-call | flops 28991029248 | bytes 50331648 | tf_op jit(solution)/shard_map/chunk_grads/pallas_call | solution.py:334
  183.3 52.7 %input_grad.2 = (bf16[8192,768]{1,0:T(8,128)(2,1)}, f32[2,192,768]{2,1,0:T(8,128)}, f32[2,192,768]{2,1,0:T(8,128)}, f32[2,192,768]{2,1,0:T(8,128)}, f32[2,192,768]{2,1,0:T(8,128)}) custom-call(bf16[8192,768]{1,0:T(8,128)(2,1)} %refs_0_.13, bf16[8192,768]{1,0:T(8,128)(2,1)} %get-tuple-element.68.refs_1_, bf16[8192,768]{1,0:T(8,128)(2,1)} %get-tuple-element.71.refs_2_, ...), custom_call_target="tpu_custom_call" | custom-call | flops 38654705664 | bytes 75497472 | tf_op jit(solution)/shard_map/input_grad/pallas_call | solution.py:390
  236.0 46.2 %chunk_grads.12 = (bf16[8192,768]{1,0:T(8,128)(2,1)}, bf16[768,768]{1,0:T(8,128)(2,1)}, bf16[768,768]{1,0:T(8,128)(2,1)}, f32[3072,768]{1,0:T(8,128)}, f32[768,3072]{1,0:T(8,128)}) custom-call(bf16[8192,3072]{1,0:T(8,128)(2,1)} %refs_0_.17, bf16[8192,768]{1,0:T(8,128)(2,1)} %get-tuple-element.85.refs_1_.refs_0_, bf16[8192,768]{1,0:T(8,128)(2,1)} %refs_2_.15, ...), custom_call_target="tpu_custom_call" | custom-call | flops 28991029248 | bytes 50331648 | tf_op jit(solution)/shard_map/chunk_grads/pallas_call | solution.py:334
  282.2 46.7 %chunk_grads.13 = (bf16[8192,768]{1,0:T(8,128)(2,1)}, bf16[768,768]{1,0:T(8,128)(2,1)}, bf16[768,768]{1,0:T(8,128)(2,1)}, f32[2,192,768]{2,1,0:T(8,128)}, f32[2,...) custom-call(bf16[8192,3072]{1,0:T(8,128)(2,1)} %refs_0_.17, ...), custom_call_target="tpu_custom_call" | custom-call | flops 28991029248 | bytes 50331648 | tf_op jit(solution)/shard_map/chunk_grads/pallas_call | solution.py:334
  328.9 46.7 %chunk_grads.14 = (bf16[8192,768]{1,0:T(8,128)(2,1)}, bf16[768,768]{1,0:T(8,128)(2,1)}, bf16[768,768]{1,0:T(8,128)(2,1)}, f32[2,192,768]{2,1,0:T(8,128)}, f32[2,...) custom-call(bf16[8192,3072]{1,0:T(8,128)(2,1)} %refs_0_.17, ...), custom_call_target="tpu_custom_call" | custom-call | flops 28991029248 | bytes 50331648 | tf_op jit(solution)/shard_map/chunk_grads/pallas_call | solution.py:334
  375.6 46.5 %chunk_grads.15 = (bf16[8192,768]{1,0:T(8,128)(2,1)}, bf16[768,768]{1,0:T(8,128)(2,1)}, bf16[768,768]{1,0:T(8,128)(2,1)}, f32[2,192,768]{2,1,0:T(8,128)}, f32[2,...) custom-call(bf16[8192,3072]{1,0:T(8,128)(2,1)} %refs_0_.17, ...), custom_call_target="tpu_custom_call" | custom-call | flops 28991029248 | bytes 50331648 | tf_op jit(solution)/shard_map/chunk_grads/pallas_call | solution.py:334
  422.0 0.0 collective-permute-start
  422.1 52.1 %input_grad.3 = (bf16[8192,768]{1,0:T(8,128)(2,1)}, f32[2,192,768]{2,1,0:T(8,128)}, f32[2,192,768]{2,1,0:T(8,128)}, f32[2,192,768]{2,1,0:T(8,128)}, f32[2,192,768]{2,1,0:T(8,128)}) custom-call(bf16[8192,768]{1,0:T(8,128)(2,1)} %get-tuple-element.85.refs_1_.refs_0_, bf16[8192,768]{1,0:T(8,128)(2,1)} %get-tuple-element.104.refs_1_, ...), custom_call_target="tpu_custom_call" | custom-call | flops 38654705664 | bytes 75497472 | tf_op jit(solution)/shard_map/input_grad/pallas_call | solution.py:390
  474.1 0.0 copy-start.1
  474.1 0.0 collective-permute-start.2
  474.2 1.4 fusion
  475.6 1.5 collective-permute-start.3
  477.1 0.5 collective-permute-start.4
  477.6 0.0 copy-done.1
  477.6 0.0 collective-permute-start.1
  477.6 0.6 pad_add_fusion.where_ref
  478.2 13.8 %place_sums.2 = (f32[3072,768]{1,0:T(8,128)}, f32[768,3072]{1,0:T(8,128)}, bf16[8192,768]{1,0:T(8,128)(2,1)}) custom-call(s32[3]{0:T(128)} %pad_add_fusion.where_ref, f32[2,192,768]{2,1,0:T(8,128)} %get-tuple-element.94.refs_0_, f32[2,192,768]{2,1,0:T(8,128)} %get-tuple-element.95.refs_1_, ...), custom_call_target="tpu_custom_call", output_to_operand_aliasing={{0}: (7, {}), {1}: (8, {})} | custom-call | flops 28991029248 | bytes 37748736 | tf_op jit(solution)/shard_map/place_sums/pallas_call | solution.py:448
  491.9 0.0 collective-permute-done.3.refs_14_
  492.0 0.5 collective-permute-done.4.refs_16_
  492.4 0.0 collective-permute-start.5
  492.5 0.5 collective-permute-start.6
  493.0 1.5 collective-permute-done.5.refs_15_
  494.4 0.0 copy-start.2
  494.5 0.8 collective-permute-done.6.refs_17_
  495.3 0.0 copy-start.3
  495.3 0.0 collective-permute-done.1.refs_11_
  495.3 0.0 collective-permute-done.2.refs_13_
  495.3 0.0 collective-permute-done.refs_10_
  495.3 0.0 copy-start
  495.3 0.0 copy-done.2
  495.3 0.8 copy-done.3
  496.1 0.4 copy-done
  496.5 13.9 %place_sums.3 = (f32[3072,768]{1,0:T(8,128)}, f32[768,3072]{1,0:T(8,128)}) custom-call(s32[3]{0:T(128)} %pad_add_fusion.where_ref, f32[2,192,768]{2,1,0:T(8,128)} %get-tuple-element.99.refs_6_.refs_7_.refs_0_, f32[2,192,768]{2,1,0:T(8,128)} %get-tuple-element.110.refs_8_.refs_1_, f32[2,192,768]{2,1,0:T(8,128)} %get-tuple-element.119.refs_2_, ...), custom_call_target="tpu_custom_call" | custom-call | flops 28991029248 | bytes 37748736 | tf_op jit(solution)/shard_map/place_sums/pallas_call | solution.py:448
Async XLA Ops:
  422.0 73.3 %collective-permute-start = (f32[2,192,768]{2,1,0:T(8,128)}, f32[2,192,768]{2,1,0:T(8,128)S(1)}, u32[]{:S(2)}, u32[]{:S(2)}) collective-permute-start(f32[2,192,768]{2,1,0:T(8,128)} %get-tuple-element.114.refs_8_), channel_id=1, source_target_pairs={{0,1},{1,0},{2,3},{3,2},{4,5},{5,4},{6,7},{7,6}} | collective-permute-start | bytes 3538952 | tf_op jit(solution)/shard_map/ppermute | solution.py:466
  474.1 3.5 copy-start.1
  474.1 21.2 %collective-permute-start.2 = (f32[2,192,768]{2,1,0:T(8,128)}, f32[2,192,768]{2,1,0:T(8,128)}, u32[]{:S(2)}, u32[]{:S(2)}) collective-permute-start(f32[2,192,768]{2,1,0:T(8,128)} %get-tuple-element.124.refs_12_), channel_id=1, source_target_pairs={{0,1},{1,0},{2,3},{3,2},{4,5},{5,4},{6,7},{7,6}} | collective-permute-start | bytes 3538952 | tf_op jit(solution)/shard_map/ppermute | solution.py:466
  475.6 16.4 %collective-permute-start.3 = (f32[1,192,768]{2,1,0:T(8,128)S(1)}, f32[1,192,768]{2,1,0:T(8,128)}, u32[]{:S(2)}, u32[]{:S(2)}) collective-permute-start(f32[1,192,768]{2,1,0:T(8,128)S(1)} %get-tuple-element.132), channel_id=1, source_target_pairs={{0,2},{2,0},{1,3},{3,1},{4,6},{6,4},{5,7},{7,5}} | collective-permute-start | bytes 1769480 | tf_op jit(solution)/shard_map/ppermute | solution.py:466
  477.1 15.4 %collective-permute-start.4 = (f32[1,192,768]{2,1,0:T(8,128)S(1)}, f32[1,192,768]{2,1,0:T(8,128)}, u32[]{:S(2)}, u32[]{:S(2)}) collective-permute-start(f32[1,192,768]{2,1,0:T(8,128)S(1)} %get-tuple-element.131), channel_id=1, source_target_pairs={{0,4},{4,0},{1,5},{5,1},{2,6},{6,2},{3,7},{7,3}} | collective-permute-start | bytes 1769480 | tf_op jit(solution)/shard_map/ppermute | solution.py:466
  477.6 17.7 %collective-permute-start.1 = (f32[2,192,768]{2,1,0:T(8,128)S(1)}, f32[2,192,768]{2,1,0:T(8,128)}, u32[]{:S(2)}, u32[]{:S(2)}) collective-permute-start(f32[2,192,768]{2,1,0:T(8,128)S(1)} %copy-done.1), channel_id=1, source_target_pairs={{0,1},{1,0},{2,3},{3,2},{4,5},{5,4},{6,7},{7,6}} | collective-permute-start | bytes 3538952 | tf_op jit(solution)/shard_map/ppermute | solution.py:466
  492.4 2.0 collective-permute-start.5
  492.5 2.8 collective-permute-start.6
  494.4 0.9 copy-start.2
  495.3 0.8 copy-start.3
  495.3 1.2 copy-start

commit v5 on v4

--- a/solution.py
+++ b/solution.py
@@ -232,17 +232,16 @@
             dst = self.sum_in.at[pl.ds(row, quarter), pl.ds(part * width, width)]
         return pltpu.make_async_copy(self.held.at[index, entry], dst, self.out_sem.at[index, entry])
 
-    def fetch(self):
-        for index in range(len(self.layout)):
-            self.load(index).start()
-
-    def place(self):
-        for index, (_, sides, own, _) in enumerate(self.layout):
-            self.load(index).wait()
-            into_out = self.first if own else jnp.logical_not(self.first)
-            for entry in range(len(sides)):
-                pl.when(into_out)(lambda: self.store(index, entry, True).start())
-                pl.when(jnp.logical_not(into_out))(lambda: self.store(index, entry, False).start())
+    def fetch(self, index):
+        self.load(index).start()
+
+    def place(self, index):
+        _, sides, own, _ = self.layout[index]
+        self.load(index).wait()
+        into_out = self.first if own else jnp.logical_not(self.first)
+        for entry in range(len(sides)):
+            pl.when(into_out)(lambda: self.store(index, entry, True).start())
+            pl.when(jnp.logical_not(into_out))(lambda: self.store(index, entry, False).start())
 
     def finish(self):
         for index, (_, sides, _, _) in enumerate(self.layout):
@@ -274,8 +273,9 @@
     if hosted:
         where = [lax.axis_index(name) for name in ('group', 'second', 'third')]
         placer = Placer(layout, where, pieces, *sums, *room)
-        pl.when(step == 2)(placer.fetch)
-        pl.when(step == 6)(placer.place)
+        for index in range(hosted):
+            pl.when(step == 1 + index)(lambda: placer.fetch(index))
+            pl.when(step == 3 + index)(lambda: placer.place(index))
         pl.when(step == pl.num_programs(0) - 1)(placer.finish)
 
     @pl.when(step == 0)
@@ -291,9 +291,8 @@
         dz = (jnp.dot(dy_ref[part, :], turned[...], preferred_element_type=jnp.float32) * slope).astype(jnp.bfloat16)
         dz_ref[part, :] = dz
         hidden_parts.append(hidden)
-        dz_parts.append(dz)
+    acc_i[...] += dot(x_ref[...], dz_ref[...], CONTRACT_ROWS)
     acc_o[...] += dot(jnp.concatenate(hidden_parts, axis=0), dy_ref[...], CONTRACT_ROWS)
-    acc_i[...] += dot(x_ref[...], jnp.concatenate(dz_parts, axis=0), CONTRACT_ROWS)
 
     @pl.when(step == pl.num_programs(0) - 1)
     def _():
@@ -418,11 +417,13 @@
         src, dst = (rows_held, rows_out) if back else (rows_in, rows_held)
         return pltpu.make_async_copy(src.at[part], dst.at[part], rows_sem.at[back, tile])
 
-    placer.fetch()
+    for index in range(len(layout)):
+        placer.fetch(index)
     if has_rows:
         for tile in range(ROW_TILES):
             row_copy(tile, 0).start()
-    placer.place()
+    for index in range(len(layout)):
+        placer.place(index)
     if has_rows:
         for tile in range(ROW_TILES):
             row_copy(tile, 0).wait()
@@ -536,11 +537,15 @@
             rest += ([] if n in own_done else own_entries(n)) + ([] if n in mate_done else mate_entries(n))
         *sums_two, dx_one = place_sums(where, rest, count, placed, dx_one)
         *sides, dx_one = lax.optimization_barrier((*sides, dx_one))
-        late = [(mine[last], count - 1, both, True, False), (mate_last, count - 1, both, False, False)]
+        ready = [entry for n in range(count, last) for entry in own_entries(n) + mate_entries(n)]
+        late = [entry for entry in ready if entry[0] is mates[last - 1][1]]
+        ready = [entry for entry in ready if entry[0] is not mates[last - 1][1]]
+        ready.append((mine[last], count - 1, both, True, False))
+        late.append((mate_last, count - 1, both, False, False))
         for side, piece in enumerate(sides):
             late += [(piece, count - 1, (side,), True, True), (flip(piece, 'group'), count - 1, (side,), False, True)]
-        ready = [entry for n in range(count, last) for entry in own_entries(n) + mate_entries(n)]
-        sums_one = place_sums(where, ready + late, count)
+        sums_one = place_sums(where, ready, count)
+        sums_one = place_sums(where, late, count, sums_one)
         return *sums_two, *sums_one, dx_one
 
     row_spec = P(AXES, None)

time: 511 us -> 496 us (0.971)
  Pallas kernels: 501 us -> 489 us
    pallas_call x8, Pallas kernels: 369 us -> 355 us  [chunk_grads(): pl.pallas_call(functools.partial(chunk_kernel, lane_plan(load), layout),...]
    pallas_call x2 -> x3, Pallas kernels: 27.7 us -> 29.1 us  [place_sums(): pl.pallas_call(functools.partial(place_kernel, layout, len(base) > 0, row...]
  transfers between devices with their start and end apart: 7 -> 7, of which waited for: 3 -> 0; matrix products, arithmetic and copies ran while one was open for 0% -> 0% of each run, Pallas kernels for 13% -> 16%
where the time goes in v5:
time: 496 us
  Pallas kernels  489 us (99%)
    pallas_call x8, Pallas kernels, chunk_grads(): pl.pallas_call(functools.partial(chunk_kernel, lane_plan(load), layout),...  355 us
    pallas_call x2, Pallas kernels, input_grad(): pl.pallas_call(functools.partial(input_kernel, lane_plan(load), len(dz_pa...  105 us
    pallas_call x3, Pallas kernels, place_sums(): pl.pallas_call(functools.partial(place_kernel, layout, len(base) > 0, row...  29.1 us
  transfers between devices with their start and end apart: 7, of which 0 were waited for; matrix products, arithmetic and copies ran while one was open for 0% of the time, Pallas kernels for 16%

profile of v5, /device:TPU:0, one launch (start us, length us, event | category | flops | bytes accessed | tf_op | source)
XLA Modules:
  0.0 495.9 jit_solution(17836083696153568067)
XLA Ops:
  0.6 39.0 %chunk_grads.8 = (bf16[8192,768]{1,0:T(8,128)(2,1)}, bf16[768,768]{1,0:T(8,128)(2,1)}, bf16[768,768]{1,0:T(8,128)(2,1)}) custom-call(bf16[8192,3072]{1,0:T(8,128)(2,1)} %refs_0_.12, bf16[8192,768]{1,0:T(8,128)(2,1)} %refs_0_.13, bf16[8192,768]{1,0:T(8,128)(2,1)} %refs_2_.11, bf16[3072,768]{1,0:T(8,128)(2,1)} %refs_3_.11), custom_call_target="tpu_custom_call" | custom-call | flops 28991029248 | bytes 50331648 | tf_op jit(solution)/shard_map/chunk_grads/pallas_call | solution.py:333
  39.6 45.0 %chunk_grads.9 = (bf16[8192,768]{1,0:T(8,128)(2,1)}, bf16[768,768]{1,0:T(8,128)(2,1)}, bf16[768,768]{1,0:T(8,128)(2,1)}, f32[2,192,768]{2,1,0:T(8,128)}) custom-call(bf16[8192,3072]{1,0:T(8,128)(2,1)} %refs_0_.12, bf16[8192,768]{1,0:T(8,128)(2,1)} %refs_0_.13, bf16[8192,768]{1,0:T(8,128)(2,1)} %refs_2_.11, bf16[3072,768]{1,0:T(8,128)(2,1)} %refs_3_.11, ...), custom_call_target="tpu_custom_call" | custom-call | flops 28991029248 | bytes 50331648 | tf_op jit(solution)/shard_map/chunk_grads/pallas_call | solution.py:333
  84.7 46.2 %chunk_grads.10 = (bf16[8192,768]{1,0:T(8,128)(2,1)}, bf16[768,768]{1,0:T(8,128)(2,1)}, bf16[768,768]{1,0:T(8,128)(2,1)}, f32[2,192,768]{2,1,0:T(8,128)}, f32[2,192,768]{2,1,0:T(8,128)}) custom-call(bf16[8192,3072]{1,0:T(8,128)(2,1)} %refs_0_.12, bf16[8192,768]{1,0:T(8,128)(2,1)} %refs_0_.13, bf16[8192,768]{1,0:T(8,128)(2,1)} %refs_2_.11, ...), custom_call_target="tpu_custom_call" | custom-call | flops 28991029248 | bytes 50331648 | tf_op jit(solution)/shard_map/chunk_grads/pallas_call | solution.py:333
  130.9 45.5 %chunk_grads.11 = (bf16[8192,768]{1,0:T(8,128)(2,1)}, bf16[768,768]{1,0:T(8,128)(2,1)}, bf16[768,768]{1,0:T(8,128)(2,1)}, f32[2,192,768]{2,1,0:T(8,128)}, f32[2,...) custom-call(bf16[8192,3072]{1,0:T(8,128)(2,1)} %refs_0_.12, bf16[8192,768]{1,0:T(8,128)(2,1)} %refs_0_.13, ...), custom_call_target="tpu_custom_call" | custom-call | flops 28991029248 | bytes 50331648 | tf_op jit(solution)/shard_map/chunk_grads/pallas_call | solution.py:333
  176.4 52.4 %input_grad.2 = (bf16[8192,768]{1,0:T(8,128)(2,1)}, f32[2,192,768]{2,1,0:T(8,128)}, f32[2,192,768]{2,1,0:T(8,128)}, f32[2,192,768]{2,1,0:T(8,128)}, f32[2,192,768]{2,1,0:T(8,128)}) custom-call(bf16[8192,768]{1,0:T(8,128)(2,1)} %refs_0_.13, bf16[8192,768]{1,0:T(8,128)(2,1)} %get-tuple-element.70.refs_1_, bf16[8192,768]{1,0:T(8,128)(2,1)} %get-tuple-element.73.refs_2_, ...), custom_call_target="tpu_custom_call" | custom-call | flops 38654705664 | bytes 75497472 | tf_op jit(solution)/shard_map/input_grad/pallas_call | solution.py:389
  228.8 41.5 %chunk_grads.12 = (bf16[8192,768]{1,0:T(8,128)(2,1)}, bf16[768,768]{1,0:T(8,128)(2,1)}, bf16[768,768]{1,0:T(8,128)(2,1)}, f32[3072,768]{1,0:T(8,128)}, f32[768,3072]{1,0:T(8,128)}) custom-call(bf16[8192,3072]{1,0:T(8,128)(2,1)} %refs_0_.17, bf16[8192,768]{1,0:T(8,128)(2,1)} %get-tuple-element.87.refs_1_.refs_0_, bf16[8192,768]{1,0:T(8,128)(2,1)} %refs_2_.15, ...), custom_call_target="tpu_custom_call" | custom-call | flops 28991029248 | bytes 50331648 | tf_op jit(solution)/shard_map/chunk_grads/pallas_call | solution.py:333
  270.3 45.5 %chunk_grads.13 = (bf16[8192,768]{1,0:T(8,128)(2,1)}, bf16[768,768]{1,0:T(8,128)(2,1)}, bf16[768,768]{1,0:T(8,128)(2,1)}, f32[2,192,768]{2,1,0:T(8,128)}, f32[2,...) custom-call(bf16[8192,3072]{1,0:T(8,128)(2,1)} %refs_0_.17, ...), custom_call_target="tpu_custom_call" | custom-call | flops 28991029248 | bytes 50331648 | tf_op jit(solution)/shard_map/chunk_grads/pallas_call | solution.py:333
  315.8 46.4 %chunk_grads.14 = (bf16[8192,768]{1,0:T(8,128)(2,1)}, bf16[768,768]{1,0:T(8,128)(2,1)}, bf16[768,768]{1,0:T(8,128)(2,1)}, f32[2,192,768]{2,1,0:T(8,128)}, f32[2,...) custom-call(bf16[8192,3072]{1,0:T(8,128)(2,1)} %refs_0_.17, ...), custom_call_target="tpu_custom_call" | custom-call | flops 28991029248 | bytes 50331648 | tf_op jit(solution)/shard_map/chunk_grads/pallas_call | solution.py:333
  362.2 45.5 %chunk_grads.15 = (bf16[8192,768]{1,0:T(8,128)(2,1)}, bf16[768,768]{1,0:T(8,128)(2,1)}, bf16[768,768]{1,0:T(8,128)(2,1)}, f32[2,192,768]{2,1,0:T(8,128)}, f32[2,...) custom-call(bf16[8192,3072]{1,0:T(8,128)(2,1)} %refs_0_.17, ...), custom_call_target="tpu_custom_call" | custom-call | flops 28991029248 | bytes 50331648 | tf_op jit(solution)/shard_map/chunk_grads/pallas_call | solution.py:333
  407.8 0.0 collective-permute-start.6
  407.8 52.5 %input_grad.3 = (bf16[8192,768]{1,0:T(8,128)(2,1)}, f32[2,192,768]{2,1,0:T(8,128)}, f32[2,192,768]{2,1,0:T(8,128)}, f32[2,192,768]{2,1,0:T(8,128)}, f32[2,192,768]{2,1,0:T(8,128)}) custom-call(bf16[8192,768]{1,0:T(8,128)(2,1)} %get-tuple-element.87.refs_1_.refs_0_, bf16[8192,768]{1,0:T(8,128)(2,1)} %get-tuple-element.106.refs_1_, ...), custom_call_target="tpu_custom_call" | custom-call | flops 38654705664 | bytes 75497472 | tf_op jit(solution)/shard_map/input_grad/pallas_call | solution.py:389
  460.3 0.0 copy-start
  460.3 0.2 collective-permute-start.1
  460.5 1.4 fusion
  462.0 0.8 collective-permute-start.2
  462.8 1.2 collective-permute-start.3
  464.0 0.0 copy-done
  464.0 0.0 collective-permute-start
  464.0 0.6 pad_add_fusion.where_ref
  464.6 13.8 %place_sums.3 = (f32[3072,768]{1,0:T(8,128)}, f32[768,3072]{1,0:T(8,128)}, bf16[8192,768]{1,0:T(8,128)(2,1)}) custom-call(s32[3]{0:T(128)} %pad_add_fusion.where_ref, f32[2,192,768]{2,1,0:T(8,128)} %get-tuple-element.96.refs_0_, f32[2,192,768]{2,1,0:T(8,128)} %get-tuple-element.97.refs_1_, ...), custom_call_target="tpu_custom_call", output_to_operand_aliasing={{0}: (7, {}), {1}: (8, {})} | custom-call | flops 28991029248 | bytes 37748736 | tf_op jit(solution)/shard_map/place_sums/pallas_call | solution.py:449
  478.4 0.0 collective-permute-done.2.refs_2_
  478.4 0.0 collective-permute-done.3.refs_4_
  478.4 0.5 collective-permute-start.4
  478.9 0.0 collective-permute-start.5
  479.0 0.0 collective-permute-done.6.refs_10_
  479.0 11.1 %place_sums.4 = (f32[3072,768]{1,0:T(8,128)}, f32[768,3072]{1,0:T(8,128)}) custom-call(s32[3]{0:T(128)} %pad_add_fusion.where_ref, f32[2,192,768]{2,1,0:T(8,128)} %get-tuple-element.101.refs_6_.refs_7_.refs_0_, f32[2,192,768]{2,1,0:T(8,128)} %get-tuple-element.112.refs_8_.refs_1_, f32[2,192,768]{2,1,0:T(8,128)} %get-tuple-element.126.refs_2_, ...), custom_call_target="tpu_custom_call" | custom-call | flops 28991029248 | bytes 37748736 | tf_op jit(solution)/shard_map/place_sums/pallas_call | solution.py:449
  490.0 0.0 collective-permute-done.4.refs_3_
  490.0 0.0 copy-start.2
  490.0 0.0 collective-permute-done.5.refs_5_
  490.1 0.0 copy-start.3
  490.1 0.0 collective-permute-done.refs_0_
  490.1 0.0 collective-permute-done.1.refs_1_
  490.1 0.0 copy-start.1
  490.1 0.7 copy-done.2
  490.8 0.2 copy-done.3
  491.1 0.4 copy-done.1
  491.4 4.3 place_sums.5
Async XLA Ops:
  407.8 71.2 %collective-permute-start.6 = (f32[2,192,768]{2,1,0:T(8,128)}, f32[2,192,768]{2,1,0:T(8,128)}, u32[]{:S(2)}, u32[]{:S(2)}) collective-permute-start(f32[2,192,768]{2,1,0:T(8,128)} %get-tuple-element.116.refs_8_), channel_id=1, source_target_pairs={{0,1},{1,0},{2,3},{3,2},{4,5},{5,4},{6,7},{7,6}} | collective-permute-start | bytes 3538952 | tf_op jit(solution)/shard_map/ppermute | solution.py:467
  460.3 3.7 copy-start
  460.3 29.8 %collective-permute-start.1 = (f32[2,192,768]{2,1,0:T(8,128)}, f32[2,192,768]{2,1,0:T(8,128)S(1)}, u32[]{:S(2)}, u32[]{:S(2)}) collective-permute-start(f32[2,192,768]{2,1,0:T(8,128)} %get-tuple-element.122.refs_11_), channel_id=1, source_target_pairs={{0,1},{1,0},{2,3},{3,2},{4,5},{5,4},{6,7},{7,6}} | collective-permute-start | bytes 3538952 | tf_op jit(solution)/shard_map/ppermute | solution.py:467
  462.0 16.4 %collective-permute-start.2 = (f32[1,192,768]{2,1,0:T(8,128)S(1)}, f32[1,192,768]{2,1,0:T(8,128)}, u32[]{:S(2)}, u32[]{:S(2)}) collective-permute-start(f32[1,192,768]{2,1,0:T(8,128)S(1)} %get-tuple-element.136), channel_id=1, source_target_pairs={{0,2},{2,0},{1,3},{3,1},{4,6},{6,4},{5,7},{7,5}} | collective-permute-start | bytes 1769480 | tf_op jit(solution)/shard_map/ppermute | solution.py:467
  462.8 15.6 %collective-permute-start.3 = (f32[1,192,768]{2,1,0:T(8,128)S(1)}, f32[1,192,768]{2,1,0:T(8,128)}, u32[]{:S(2)}, u32[]{:S(2)}) collective-permute-start(f32[1,192,768]{2,1,0:T(8,128)S(1)} %get-tuple-element.135), channel_id=1, source_target_pairs={{0,4},{4,0},{1,5},{5,1},{2,6},{6,2},{3,7},{7,3}} | collective-permute-start | bytes 1769480 | tf_op jit(solution)/shard_map/ppermute | solution.py:467
  464.0 26.1 %collective-permute-start = (f32[2,192,768]{2,1,0:T(8,128)S(1)}, f32[2,192,768]{2,1,0:T(8,128)}, u32[]{:S(2)}, u32[]{:S(2)}) collective-permute-start(f32[2,192,768]{2,1,0:T(8,128)S(1)} %copy-done), channel_id=1, source_target_pairs={{0,1},{1,0},{2,3},{3,2},{4,5},{5,4},{6,7},{7,6}} | collective-permute-start | bytes 3538952 | tf_op jit(solution)/shard_map/ppermute | solution.py:467
  478.4 11.6 %collective-permute-start.4 = (f32[1,192,768]{2,1,0:T(8,128)}, f32[1,192,768]{2,1,0:T(8,128)S(1)}, u32[]{:S(2)}, u32[]{:S(2)}) collective-permute-start(f32[1,192,768]{2,1,0:T(8,128)} %collective-permute-done.2.refs_2_), channel_id=1, source_target_pairs={{0,1},{1,0},{2,3},{3,2},{4,5},{5,4},{6,7},{7,6}} | collective-permute-start | bytes 1769480 | tf_op jit(solution)/shard_map/ppermute | solution.py:467
  478.9 11.1 %collective-permute-start.5 = (f32[1,192,768]{2,1,0:T(8,128)}, f32[1,192,768]{2,1,0:T(8,128)S(1)}, u32[]{:S(2)}, u32[]{:S(2)}) collective-permute-start(f32[1,192,768]{2,1,0:T(8,128)} %collective-permute-done.3.refs_4_), channel_id=1, source_target_pairs={{0,1},{1,0},{2,3},{3,2},{4,5},{5,4},{6,7},{7,6}} | collective-permute-start | bytes 1769480 | tf_op jit(solution)/shard_map/ppermute | solution.py:467
  490.0 0.8 copy-start.2
  490.1 1.0 copy-start.3
  490.1 1.3 copy-start.1
